TPU v7x, 32 devices: a whole 2x2x4 slice. The times are simulated.
32 devices in a mesh: dp: 4 (over y, core), expert: 4 (over z), tensor: 2 (over x).
Axes of the slice: x: 2, y: 2, z: 4, core: 2. Of those that a mesh axis runs over, the one named last changes fastest.
Arguments:
- router_input: bfloat16 [1024, 2048], P(('dp', 'expert'), 'tensor'), may hold values from -6 to 6
- router_weight: bfloat16 [2048, 8], replicated, may hold values from -0.125 to 0.125
- expert_ids: int32 [1024, 2], P(('dp', 'expert', 'tensor')), may hold values from 0 to 7, all different within a row; in each aligned block of 32 rows (0 to 31, 32 to 63, ...) at most 9 rows name the same one
- down_weight: bfloat16 [61440, 2048], P(('expert', 'tensor')), may hold values from -0.0625 to 0.0625
- hidden: bfloat16 [4, 72, 61440], P('dp', None, ('expert', 'tensor')), may hold values from -6 to 6
- grad_output: bfloat16 [1024, 2048], P(('dp', 'expert', 'tensor')), may hold values from -4 to 4
Outputs:
- weight_grad: bfloat16 [61440, 2048], P(('expert', 'tensor', 'dp'))
- hidden_grad: bfloat16 [4, 72, 61440], P('dp', None, ('expert', 'tensor'))
- router_grad: float32 [2048, 8], replicated
- input_grad: bfloat16 [1024, 2048], P(('dp', 'expert', 'tensor'))
Inputs may be any that keep to these rules, and one draw needn't show every extreme that they name: `expert_ids`: each row names 2 different experts. Within the 32 rows of one device no expert is named more than 9 times, and some device's rows name some expert exactly 9 times.
All inputs are finite; a program needn't handle non-finite values.
Results may differ from a plain program's by a relative error of at most 0.018.
Values may be sent and summed in bfloat16 or wider, within the bound.
A program may use at most 192 MiB of HBM per device.

v0:
```python
import functools

import jax
import jax.numpy as jnp
from jax import lax
from jax.experimental import pallas as pl
from jax.experimental.pallas import tpu as pltpu
from jax.sharding import PartitionSpec as P


PAD = 16
PIECES = 4
LANES = 128
VMEM_LIMIT = 64 * 1000 * 1000
EXACT = lax.Precision.HIGHEST
CONTRACT_LAST = (((1,), (1,)), ((), ()))
CONTRACT_FIRST = (((0,), (0,)), ((), ()))


def iota(shape, axis):
    return lax.broadcasted_iota(jnp.int32, shape, axis)


def exchange_kernel(
    groups, expert_ranks, tensor_ranks, capacity, tile,
    ids_ref, router_weight_ref, grad_ref, router_input_ref, down_ref, hidden_ref,
    hidden_grad_ref, input_grad_ref, router_grad_ref, hidden_all_ref, gated_out_ref,
    weights, hidden_rows, full_input, send_grad, recv_grad, send_gate, recv_gate,
    send_back, recv_back, send_sum, recv_sum, packed, gate_acc, gated_all_ref, hidden_out, image_acc,
    weight_sem, hidden_sem, own_sem, piece_sem, out_sem, gated_out,
    input_send, input_recv, hidden_send, hidden_recv, grad_send, grad_recv,
    gate_send, gate_recv, gated_send, gated_recv, back_send, back_recv,
    sum_send, sum_recv, whole_send, whole_recv,
):
    f32, bf16 = jnp.float32, jnp.bfloat16
    group = lax.axis_index("dp")
    tensor = lax.axis_index("tensor")
    sources = expert_ranks * tensor_ranks
    source = lax.axis_index("expert") * tensor_ranks + tensor
    devices = groups * sources
    me = group * sources + source
    slots, width = hidden_ref.shape
    part = width // groups
    experts = router_weight_ref.shape[0]
    tokens = grad_ref.shape[0]
    span = router_input_ref.shape[1]
    rows = sources * PAD
    tiles = width // tile

    def place(d, x):
        return {"dp": d, "expert": x // tensor_ranks, "tensor": x % tensor_ranks}

    def remote(src, dst, send, recv, device):
        return pltpu.make_async_remote_copy(
            src_ref=src, dst_ref=dst, send_sem=send, recv_sem=recv,
            device_id=device, device_id_type=pl.DeviceIdType.MESH,
        )

    def weight_copy(i):
        return pltpu.make_async_copy(
            down_ref.at[pl.ds(i * tile, tile)], weights.at[i], weight_sem.at[i]
        )

    barrier = pltpu.get_barrier_semaphore()

    @pl.loop(1, devices)
    def _(k):
        other = (me + k) % devices
        pl.semaphore_signal(
            barrier, inc=1, device_id=place(other // sources, other % sources),
            device_id_type=pl.DeviceIdType.MESH,
        )

    hidden_load = pltpu.make_async_copy(hidden_ref, hidden_rows, hidden_sem)
    hidden_load.start()

    @pl.loop(0, tiles)
    def _(i):
        weight_copy(i).start()

    labels = iota((experts, tokens), 0)
    same = (iota((tokens, tokens), 0) == iota((tokens, tokens), 1)).astype(f32)
    first = lax.dot_general(
        same, (ids_ref[0:1, :] == labels).astype(f32), CONTRACT_LAST, preferred_element_type=f32
    )
    second = lax.dot_general(
        same, (ids_ref[1:2, :] == labels).astype(f32), CONTRACT_LAST, preferred_element_type=f32
    )
    both = first + second
    earlier = (iota((tokens, tokens), 1) < iota((tokens, tokens), 0)).astype(f32)
    before = jnp.dot(earlier, both, preferred_element_type=f32)
    spread_rows = ((iota((rows, experts), 0) >> 4) == iota((rows, experts), 1)).astype(f32)
    hit = lax.dot_general(spread_rows, both, CONTRACT_LAST, preferred_element_type=f32)
    rank = lax.dot_general(spread_rows, before, CONTRACT_LAST, preferred_element_type=f32)
    slot = (iota((rows, tokens), 0) & (PAD - 1)).astype(f32)
    table = jnp.where((hit > 0.5) & (jnp.abs(rank - slot) < 0.5), 1.0, 0.0).astype(f32)
    wide = grad_ref.shape[1] // PIECES
    for p in range(PIECES):
        send_grad[p] = (
            jnp.dot(
                table.astype(bf16), grad_ref[:, p * wide : (p + 1) * wide],
                preferred_element_type=f32,
            )
            .astype(bf16)
            .reshape(send_grad.shape[1:])
        )

    pl.semaphore_wait(barrier, devices - 1)

    grad_copies = []

    def dispatch(p):
        for k in range(1, sources):
            to = (source + k) % sources
            copy = remote(
                send_grad.at[p, to], recv_grad.at[p, source], grad_send.at[p * sources + k],
                grad_recv.at[p * sources + source], place(group, to),
            )
            copy.start()
            grad_copies.append(copy)
        own = pltpu.make_async_copy(
            send_grad.at[p, source], recv_grad.at[p, source], piece_sem.at[p]
        )
        own.start()
        return own

    own_grads = [dispatch(0)]
    input_copies = []
    for k in range(1, tensor_ranks):
        to = (tensor + k) % tensor_ranks
        copy = remote(
            router_input_ref.at[pl.ds(pl.multiple_of(to * tokens, tokens), tokens)],
            full_input.at[tensor], input_send.at[k], input_recv.at[tensor],
            {"tensor": to},
        )
        copy.start()
        input_copies.append(copy)
    own_input = pltpu.make_async_copy(
        router_input_ref.at[pl.ds(pl.multiple_of(tensor * tokens, tokens), tokens)],
        full_input.at[tensor], own_sem.at[0],
    )
    own_input.start()

    for p in range(1, PIECES):
        own_grads.append(dispatch(p))

    hidden_copies = []
    for k in range(1, groups):
        to = (group + k) % groups
        copy = remote(
            hidden_ref.at[:, pl.ds(pl.multiple_of(to * part, LANES), part)],
            hidden_all_ref.at[group], hidden_send.at[k], hidden_recv.at[group],
            {"dp": to},
        )
        copy.start()
        hidden_copies.append(copy)

    column = iota((slots, rows), 1)
    column_slot = column & (PAD - 1)
    pick = (
        (iota((slots, rows), 0) == capacity * (column >> 4) + column_slot)
        & (column_slot < capacity)
    ).astype(f32)
    pick_low = pick.astype(bf16)

    def receive(p):
        own_grads[p].wait()
        for k in range(1, sources):
            origin = (source + k) % sources
            remote(
                send_grad.at[p, 0], recv_grad.at[p, origin], grad_send.at[p * sources + k],
                grad_recv.at[p * sources + origin], place(group, origin),
            ).wait_recv()
        packed[p] = jnp.dot(
            pick_low, recv_grad[p].reshape(rows, wide), preferred_element_type=f32
        ).astype(bf16)

    def image_piece(p, i):
        return lax.dot_general(
            packed[p], weights[i, :, p * wide : (p + 1) * wide], CONTRACT_LAST,
            preferred_element_type=f32,
        )

    receive(0)

    @pl.loop(0, tiles)
    def _(i):
        weight_copy(i).wait()
        image_acc[i] = image_piece(0, i)

    own_input.wait()
    for k in range(1, tensor_ranks):
        origin = (tensor + k) % tensor_ranks
        remote(
            router_input_ref.at[pl.ds(0, tokens)], full_input.at[origin], input_send.at[k],
            input_recv.at[origin], {"tensor": origin},
        ).wait_recv()
    logits = jnp.zeros((tokens, experts), f32)
    for h in range(tensor_ranks):
        logits = logits + lax.dot_general(
            full_input[h], router_weight_ref[:, h * span : (h + 1) * span], CONTRACT_LAST,
            preferred_element_type=f32,
        )
    chosen = jnp.sum(first * logits, axis=1, keepdims=True)
    rival = jnp.sum(second * logits, axis=1, keepdims=True)
    first_gate = jax.nn.sigmoid(chosen - rival)
    second_gate = jax.nn.sigmoid(rival - chosen)
    gates = first * first_gate + second * second_gate
    low = gates.astype(bf16).astype(f32)
    gate_rows = lax.dot_general(
        spread_rows, low, CONTRACT_LAST, preferred_element_type=f32
    )
    slot_gate = jnp.sum(table * gate_rows, axis=1, keepdims=True)
    send_gate[...] = jnp.broadcast_to(slot_gate, (rows, LANES)).reshape(send_gate.shape)
    gate_copies = []
    for k in range(1, sources):
        to = (source + k) % sources
        copy = remote(
            send_gate.at[to], recv_gate.at[source], gate_send.at[k], gate_recv.at[source],
            place(group, to),
        )
        copy.start()
        gate_copies.append(copy)
    own_gate = pltpu.make_async_copy(send_gate.at[source], recv_gate.at[source], own_sem.at[2])
    own_gate.start()

    for p in range(1, PIECES - 1):
        receive(p)

        @pl.loop(0, tiles)
        def _(i):
            image_acc[i] += image_piece(p, i)

    receive(PIECES - 1)
    own_gate.wait()
    for k in range(1, sources):
        origin = (source + k) % sources
        remote(
            send_gate.at[0], recv_gate.at[origin], gate_send.at[k], gate_recv.at[origin],
            place(group, origin),
        ).wait_recv()
    gate_lanes = jnp.dot(
        pick_low, recv_gate[...].reshape(rows, LANES).astype(bf16), preferred_element_type=f32
    )
    gate_column = gate_lanes[:, 0:1]
    for p in range(PIECES):
        gated_all_ref[pl.ds(group, 1), :, p * wide : (p + 1) * wide] = (
            gate_column * packed[p].astype(f32)
        ).astype(bf16)[None]

    core = group % 2
    half = group // 2
    beside = half * 2 + (1 - core)
    across = (1 - half) * 2 + core
    diagonal = (1 - half) * 2 + (1 - core)
    mine = gated_all_ref.at[group]
    to_across = remote(mine, mine, gated_send.at[0], gated_recv.at[group], {"dp": across})
    to_across.start()
    to_beside = remote(mine, mine, gated_send.at[1], gated_recv.at[group], {"dp": beside})
    to_beside.start()

    def gated_copy(d):
        return pltpu.make_async_copy(gated_all_ref.at[d], gated_out_ref.at[d], gated_out.at[d])

    gated_copy(group).start()
    hidden_load.wait()
    own_hidden = pltpu.make_async_copy(
        hidden_rows.at[:, pl.ds(pl.multiple_of(group * part, LANES), part)],
        hidden_all_ref.at[group], own_sem.at[3],
    )
    own_hidden.start()
    gate_acc[...] = jnp.zeros_like(gate_acc)

    @pl.loop(0, tiles)
    def _(i):
        at = pl.ds(pl.multiple_of(i * tile, tile), tile)
        image = image_acc[i] + image_piece(PIECES - 1, i)
        hidden_out[:, at] = (gate_column * image).astype(bf16)
        product = hidden_rows[:, at].astype(f32) * image
        total = product[:, 0:LANES]
        for j in range(1, tile // LANES):
            total = total + product[:, j * LANES : (j + 1) * LANES]
        gate_acc[...] += total

    hidden_store = pltpu.make_async_copy(hidden_out, hidden_grad_ref, out_sem)
    hidden_store.start()
    partial = jnp.broadcast_to(
        jnp.sum(gate_acc[...], axis=1, keepdims=True), (slots, LANES)
    )
    send_back[...] = lax.dot_general(
        pick, partial, CONTRACT_FIRST, precision=EXACT, preferred_element_type=f32
    ).reshape(send_back.shape)
    back_copies = []
    for k in range(1, sources):
        to = (source + k) % sources
        copy = remote(
            send_back.at[to], recv_back.at[source], back_send.at[k], back_recv.at[source],
            place(group, to),
        )
        copy.start()
        back_copies.append(copy)
    own_back = pltpu.make_async_copy(send_back.at[source], recv_back.at[source], own_sem.at[4])
    own_back.start()

    theirs = gated_all_ref.at[across]
    remote(theirs, theirs, gated_send.at[0], gated_recv.at[across], {"dp": across}).wait_recv()
    relay = remote(theirs, theirs, gated_send.at[2], gated_recv.at[across], {"dp": beside})
    relay.start()
    gated_copy(across).start()

    own_back.wait()
    for k in range(1, sources):
        origin = (source + k) % sources
        remote(
            send_back.at[0], recv_back.at[origin], back_send.at[k], back_recv.at[origin],
            place(group, origin),
        ).wait_recv()
    returned = recv_back[...].reshape(rows, LANES)[:, 0:1]
    gate_grad = lax.dot_general(
        table * returned, spread_rows, CONTRACT_FIRST, precision=EXACT, preferred_element_type=f32
    )
    mixed = jnp.sum(gates * gate_grad, axis=1, keepdims=True)
    logit_grad = gates * (gate_grad - mixed)
    chunk = experts // groups
    block = (span * tensor_ranks) // sources
    for h in range(tensor_ranks):
        local = lax.dot_general(
            logit_grad, full_input[h].astype(f32), CONTRACT_FIRST, precision=EXACT,
            preferred_element_type=f32,
        )
        for b in range(span // block):
            x = h * (span // block) + b
            for d in range(groups):
                send_sum[d * sources + x] = local[
                    d * chunk : (d + 1) * chunk, b * block : (b + 1) * block
                ]

    def sum_copy(k, to, slot_at):
        return remote(
            send_sum.at[to], recv_sum.at[slot_at], sum_send.at[k], sum_recv.at[slot_at],
            place(to // sources, to % sources),
        )

    def whole_copy(k, to, slot_at):
        return remote(
            router_grad_ref.at[slot_at], router_grad_ref.at[slot_at], whole_send.at[k],
            whole_recv.at[slot_at], place(to // sources, to % sources),
        )

    @pl.loop(1, devices)
    def _(k):
        sum_copy(k, (me + k) % devices, me).start()

    recv_sum[pl.ds(me, 1)] = send_sum[pl.ds(me, 1)]
    input_grad_ref[...] = jnp.dot(
        logit_grad, router_weight_ref[...].astype(f32), precision=EXACT,
        preferred_element_type=f32,
    ).astype(bf16)

    @pl.loop(1, devices)
    def _(k):
        origin = (me + k) % devices
        sum_copy(k, origin, origin).wait_recv()

    router_grad_ref[pl.ds(me, 1)] = jnp.sum(recv_sum[...], axis=0, keepdims=True)

    @pl.loop(1, devices)
    def _(k):
        whole_copy(k, (me + k) % devices, me).start()

    @pl.loop(1, devices)
    def _(k):
        origin = (me + k) % devices
        whole_copy(k, origin, origin).wait_recv()

    own_hidden.wait()
    for k in range(1, groups):
        origin = (group + k) % groups
        remote(
            hidden_ref.at[:, pl.ds(0, part)], hidden_all_ref.at[origin], hidden_send.at[k],
            hidden_recv.at[origin], {"dp": origin},
        ).wait_recv()
    for origin in (beside, diagonal):
        slab = gated_all_ref.at[origin]
        remote(
            slab, slab, gated_send.at[1], gated_recv.at[origin], {"dp": beside}
        ).wait_recv()
        gated_copy(origin).start()
    for copy in input_copies + grad_copies + hidden_copies + gate_copies + back_copies:
        copy.wait_send()
    for copy in (to_across, to_beside, relay):
        copy.wait_send()
    for d in (group, beside, across, diagonal):
        gated_copy(d).wait()
    hidden_store.wait()

    @pl.loop(1, devices)
    def _(k):
        sum_copy(k, (me + k) % devices, me).wait_send()
        whole_copy(k, (me + k) % devices, me).wait_send()


def weight_kernel(
    sources, hidden_ref, gated_ref, hidden_grad_ref, input_grad_ref, router_ref,
    out_ref, hidden_grad_out, input_grad_out, router_out,
):
    hidden_grad_out[...] = hidden_grad_ref[...]

    @pl.when(pl.program_id(0) == 0)
    def _():
        input_grad_out[...] = input_grad_ref[...]
        pieces, chunk, block = router_ref.shape
        for piece in range(pieces):
            d, x = piece // sources, piece % sources
            router_out[d * chunk : (d + 1) * chunk, x * block : (x + 1) * block] = router_ref[
                piece
            ]

    out_ref[...] = lax.dot_general(
        hidden_ref[...], gated_ref[...], CONTRACT_FIRST, preferred_element_type=jnp.float32
    ).astype(out_ref.dtype)


def by_kernels(router_input, router_weight, expert_ids, down_weight, hidden, grad_output):
    f32, bf16 = jnp.float32, jnp.bfloat16
    tokens, model = grad_output.shape
    experts = router_weight.shape[1]
    groups = lax.axis_size("dp")
    expert_ranks = lax.axis_size("expert")
    tensor_ranks = lax.axis_size("tensor")
    sources = expert_ranks * tensor_ranks
    devices = groups * sources
    slots, width = hidden.shape[1:]
    tile = tile_of(width)
    span = router_input.shape[1]
    part = width // groups
    vmem = pl.BlockSpec(memory_space=pltpu.VMEM)
    hbm = pl.BlockSpec(memory_space=pl.ANY)
    dma = pltpu.SemaphoreType.DMA
    piece = (devices, experts // groups, model // sources)
    hidden_grad, input_grad, router_parts, hidden_all, gated_all = pl.pallas_call(
        functools.partial(
            exchange_kernel, groups, expert_ranks, tensor_ranks, slots // sources, tile
        ),
        out_shape=(
            jax.ShapeDtypeStruct((slots, width), bf16),
            jax.ShapeDtypeStruct((tokens, model), bf16),
            jax.ShapeDtypeStruct(piece, f32),
            jax.ShapeDtypeStruct((groups, slots, part), bf16),
            jax.ShapeDtypeStruct((groups, slots, model), bf16),
        ),
        in_specs=[vmem, vmem, vmem, vmem, hbm, hbm],
        out_specs=(hbm, vmem, vmem, hbm, hbm),
        scratch_shapes=[
            pltpu.VMEM((width // tile, tile, model), bf16),
            pltpu.VMEM((slots, width), bf16),
            pltpu.VMEM((tensor_ranks, tokens, span), bf16),
            pltpu.VMEM((PIECES, sources, PAD, model // PIECES), bf16),
            pltpu.VMEM((PIECES, sources, PAD, model // PIECES), bf16),
            pltpu.VMEM((sources, PAD, LANES), f32),
            pltpu.VMEM((sources, PAD, LANES), f32),
            pltpu.VMEM((sources, PAD, LANES), f32),
            pltpu.VMEM((sources, PAD, LANES), f32),
            pltpu.VMEM(piece, f32),
            pltpu.VMEM(piece, f32),
            pltpu.VMEM((PIECES, slots, model // PIECES), bf16),
            pltpu.VMEM((slots, LANES), f32),
            pltpu.VMEM((groups, slots, model), bf16),
            pltpu.VMEM((slots, width), bf16),
            pltpu.VMEM((width // tile, slots, tile), f32),
            dma((width // tile,)),
            dma,
            dma((5,)),
            dma((PIECES,)),
            dma,
            dma((groups,)),
            dma((tensor_ranks,)), dma((tensor_ranks,)),
            dma((groups,)), dma((groups,)),
            dma((PIECES * sources,)), dma((PIECES * sources,)),
            dma((sources,)), dma((sources,)),
            dma((3,)), dma((groups,)),
            dma((sources,)), dma((sources,)),
            dma((devices,)), dma((devices,)),
            dma((devices,)), dma((devices,)),
        ],
        compiler_params=pltpu.CompilerParams(
            collective_id=0, has_side_effects=True, vmem_limit_bytes=VMEM_LIMIT
        ),
        name="exchange",
    )(expert_ids.T, router_weight.T, grad_output, router_input, down_weight, hidden[0])
    step = 384 if part % 384 == 0 else LANES
    steps = part // step
    slab = width // steps
    weight_grad, hidden_grad, input_grad, router_grad = pl.pallas_call(
        functools.partial(weight_kernel, sources),
        out_shape=(
            jax.ShapeDtypeStruct((part, model), bf16),
            jax.ShapeDtypeStruct((slots, width), bf16),
            jax.ShapeDtypeStruct((tokens, model), bf16),
            jax.ShapeDtypeStruct((experts, model), f32),
        ),
        grid=(steps,),
        in_specs=[
            pl.BlockSpec((groups * slots, step), lambda i: (0, i)),
            pl.BlockSpec((groups * slots, model), lambda i: (0, 0)),
            pl.BlockSpec((slots, slab), lambda i: (0, i)),
            pl.BlockSpec((tokens, model), lambda i: (0, 0)),
            pl.BlockSpec(piece, lambda i: (0, 0, 0)),
        ],
        out_specs=(
            pl.BlockSpec((step, model), lambda i: (i, 0)),
            pl.BlockSpec((slots, slab), lambda i: (0, i)),
            pl.BlockSpec((tokens, model), lambda i: (0, 0)),
            pl.BlockSpec((experts, model), lambda i: (0, 0)),
        ),
        name="weight_grad",
    )(
        hidden_all.reshape(groups * slots, part),
        gated_all.reshape(groups * slots, model),
        hidden_grad, input_grad, router_parts,
    )
    return weight_grad, hidden_grad[None], router_grad.T, input_grad


def tile_of(width):
    for tile in (512, 384, 256):
        if width % tile == 0:
            return tile
    return LANES


def kernels_fit(router_input, router_weight, expert_ids, down_weight, hidden, grad_output):
    groups = lax.axis_size("dp")
    sources = lax.axis_size("expert") * lax.axis_size("tensor")
    slots, width = hidden.shape[1:]
    tokens, model = grad_output.shape
    experts = router_weight.shape[1]
    return (
        groups == 4
        and sources == experts
        and experts % groups == 0
        and slots % 8 == 0
        and slots // sources <= PAD
        and tokens % 16 == 0
        and width % (groups * LANES) == 0
        and model % (sources * LANES) == 0
        and model % (PIECES * LANES) == 0
        and 2 * (width * model + 4 * slots * width + 8 * slots * model) < 48 * 1000 * 1000
    )


def per_device(*arrays):
    return by_kernels(*arrays) if kernels_fit(*arrays) else by_collectives(*arrays)


def by_collectives(router_input, router_weight, expert_ids, down_weight, hidden, grad_output):
    token_rows = grad_output.shape[0]
    model_width = grad_output.shape[1]
    expert_count = router_weight.shape[1]
    choose_count = expert_ids.shape[1]
    expert_ranks = lax.axis_size("expert")
    tensor_ranks = lax.axis_size("tensor")
    sources = expert_ranks * tensor_ranks
    spread = sources // expert_count
    capacity = hidden.shape[1] // sources
    full_input = lax.all_to_all(router_input, "tensor", split_axis=0, concat_axis=1, tiled=True)
    logits = jnp.dot(full_input, router_weight, preferred_element_type=jnp.float32)
    labels = jnp.arange(expert_count, dtype=jnp.int32)
    onehot_int = (expert_ids[:, :, None] == labels).astype(jnp.int32)
    onehot = onehot_int.astype(jnp.float32)
    picked = jnp.sum(onehot * logits[:, None, :], axis=2)
    first_gate = jax.nn.sigmoid(picked[:, 0] - picked[:, 1])
    second_gate = jax.nn.sigmoid(picked[:, 1] - picked[:, 0])
    gate_values = jnp.stack([first_gate, second_gate], axis=1)
    gate_low = gate_values.astype(jnp.bfloat16)
    flat_hits = onehot_int.reshape(token_rows * choose_count, expert_count)
    before = jnp.cumsum(flat_hits, axis=0) - flat_hits
    slot_pos = jnp.sum(before * flat_hits, axis=1).reshape(token_rows, choose_count)
    slot_ids = jnp.arange(capacity, dtype=jnp.int32)
    dispatch_table = onehot[:, :, :, None] * (slot_pos[:, :, None, None] == slot_ids).astype(
        jnp.float32
    )
    slot_table = jnp.sum(dispatch_table, axis=1).astype(jnp.bfloat16)
    packed_grad = jnp.einsum(
        "rec,rd->ecd", slot_table, grad_output, preferred_element_type=jnp.float32
    ).astype(jnp.bfloat16)
    packed_gate = jnp.einsum("rkec,rk->ec", dispatch_table, gate_low.astype(jnp.float32)).astype(
        jnp.bfloat16
    )
    send_grad = jnp.repeat(packed_grad, spread, axis=0)
    send_gate = jnp.repeat(packed_gate, spread, axis=0)
    recv_grad, recv_gate = (
        lax.all_to_all(send_grad, ("expert", "tensor"), split_axis=0, concat_axis=0, tiled=True),
        lax.all_to_all(send_gate, ("expert", "tensor"), split_axis=0, concat_axis=0, tiled=True),
    )
    recv_grad = recv_grad.reshape(sources * capacity, model_width)
    recv_gate = recv_gate.reshape(sources * capacity).astype(jnp.float32)
    hidden_rows = hidden[0]
    gated_grad = (recv_gate[:, None] * recv_grad.astype(jnp.float32)).astype(jnp.bfloat16)
    expert_image = lax.dot_general(
        recv_grad, down_weight, (((1,), (1,)), ((), ())), preferred_element_type=jnp.float32
    )
    hidden_part = (recv_gate[:, None] * expert_image).astype(jnp.bfloat16)
    gate_partial = jnp.sum(hidden_rows.astype(jnp.float32) * expert_image, axis=1).reshape(
        sources, capacity
    )
    returned = lax.all_to_all(
        gate_partial, ("expert", "tensor"), split_axis=0, concat_axis=0, tiled=True
    )
    expert_sums = jnp.sum(returned.reshape(expert_count, spread, capacity), axis=1)
    gate_grad = jnp.einsum("rkec,ec->rk", dispatch_table, expert_sums)
    mixed_term = jnp.sum(gate_values * gate_grad, axis=1, keepdims=True)
    logit_part = gate_values * (gate_grad - mixed_term)
    logit_grad = jnp.sum(onehot * logit_part[:, :, None], axis=1)
    input_grad = jnp.dot(
        logit_grad, router_weight.astype(jnp.float32).T, precision=lax.Precision.HIGHEST
    ).astype(jnp.bfloat16)
    router_local = jnp.dot(
        full_input.astype(jnp.float32).T, logit_grad, precision=lax.Precision.HIGHEST
    )
    router_grad = lax.psum(router_local, ("dp", "expert", "tensor"))
    hidden_all = lax.all_to_all(hidden_rows, "dp", split_axis=1, concat_axis=0, tiled=True)
    gated_all = lax.all_gather(gated_grad, "dp", axis=0, tiled=True)
    weight_sum = lax.dot_general(
        hidden_all, gated_all, (((0,), (0,)), ((), ())), preferred_element_type=jnp.float32
    ).astype(jnp.bfloat16)
    return (weight_sum, hidden_part[None], router_grad, input_grad)


def solution(mesh):
    return jax.shard_map(
        per_device,
        mesh=mesh,
        in_specs=(
            P(("dp", "expert"), "tensor"),
            P(),
            P(("dp", "expert", "tensor"), None),
            P(("expert", "tensor"), None),
            P("dp", None, ("expert", "tensor")),
            P(("dp", "expert", "tensor"), None),
        ),
        out_specs=(
            P(("expert", "tensor", "dp"), None),
            P("dp", None, ("expert", "tensor")),
            P(),
            P(("dp", "expert", "tensor"), None),
        ),
        check_vma=False,
    )
```

profile of v0, /device:TPU:0, one launch (start us, length us, event | category | flops | bytes accessed | tf_op | source)
XLA Modules:
  0.0 62.7 jit_solution(12733066151354954859)
XLA Ops:
  0.6 53.0 %exchange.1 = (bf16[72,7680]{1,0:T(8,128)(2,1)}, bf16[32,2048]{1,0:T(8,128)(2,1)}, f32[32,2,256]{2,1,0:T(2,128)}, bf16[4,72,1920]{2,1,0:T(8,128)(2,1)}, bf16[4,72,2048]{2,1,0:T(8,128)(2,1)}) custom-call(s32[2,32]{1,0:T(2,128)} %bitcast.11, bf16[8,2048]{1,0:T(8,128)(2,1)} %bitcast.10, bf16[32,2048]{1,0:T(8,128)(2,1)} %grad_ref.1, ...), custom_call_target="tpu_custom_call" | custom-call | tf_op jit(solution)/shard_map/exchange/pallas_call | solution.py:441
  53.7 9.0 %weight_grad.1 = (bf16[1920,2048]{1,0:T(8,128)(2,1)}, bf16[72,7680]{1,0:T(8,128)(2,1)}, bf16[32,2048]{1,0:T(8,128)(2,1)}, f32[8,2048]{1,0:T(8,128)}) custom-call(bf16[288,1920]{1,0:T(8,128)(2,1)} %bitcast.9, bf16[288,2048]{1,0:T(8,128)(2,1)} %bitcast.7, bf16[72,7680]{1,0:T(8,128)(2,1)} %get-tuple-element.15.hidden_grad_ref, ...), custom_call_target="tpu_custom_call" | custom-call | tf_op jit(solution)/shard_map/weight_grad/pallas_call | solution.py:494
where the time goes:
time: 62.9 us; the launch traced here: 62.7 us
  Pallas kernels  62 us (99%)
  between operations  0.64 us (1%)
    pallas_call x1, Pallas kernels, by_kernels(): pl.pallas_call(functools.partial(exchange_kernel, groups, expert_ranks, t...  53 us
    pallas_call x1, Pallas kernels, by_kernels(): pl.pallas_call(functools.partial(weight_kernel, sources), out_shape=(jax....  9 us

commit v1 on v0

v1 whole, which is shorter than its diff:
```python
import functools

import jax
import jax.numpy as jnp
from jax import lax
from jax.experimental import pallas as pl
from jax.experimental.pallas import tpu as pltpu
from jax.sharding import PartitionSpec as P


PAD = 16
LANES = 128
HALF = 8
VMEM_LIMIT = 54 * 1000 * 1000
STORE_LIMIT = 8 * 1000 * 1000
OUT = pltpu.VMEM
EXACT = lax.Precision.HIGHEST
CONTRACT_LAST = (((1,), (1,)), ((), ()))
CONTRACT_FIRST = (((0,), (0,)), ((), ()))


def iota(shape, axis):
    return lax.broadcasted_iota(jnp.int32, shape, axis)


def exchange_kernel(
    groups, expert_ranks, tensor_ranks, capacity, tile,
    ids_hbm, router_weight_hbm, grad_hbm, router_input_ref, down_ref, hidden_ref,
    weight_grad_ref, hidden_out, input_grad_ref, router_grad_ref,
    ids_ref, router_weight_ref, grad_ref, full_input, weights, hidden_rows,
    send_low, recv_low, send_top, recv_top, send_gate, recv_gate, send_back, recv_back,
    send_sum, recv_sum, packed, pulled, hidden_near, gated_near, hidden_far, gated_far,
    load_sem, weight_sem, hidden_sem, own_sem,
    input_send, input_recv, low_send, low_recv, top_send, top_recv, gate_send, gate_recv,
    hidden_send, hidden_recv, gated_send, gated_recv, back_send, back_recv,
    sum_send, sum_recv, whole_send, whole_recv,
):
    f32, bf16 = jnp.float32, jnp.bfloat16
    group = lax.axis_index("dp")
    expert = lax.axis_index("expert")
    tensor = lax.axis_index("tensor")
    sources = expert_ranks * tensor_ranks
    source = expert * tensor_ranks + tensor
    devices = groups * sources
    me = group * sources + source
    slots, width = hidden_ref.shape
    part = width // groups
    experts = router_weight_ref.shape[0]
    tokens = grad_ref.shape[0]
    span = router_input_ref.shape[1]
    rows = sources * PAD
    tiles = width // tile

    def remote(src, dst, send, recv, device):
        return pltpu.make_async_remote_copy(
            src_ref=src, dst_ref=dst, send_sem=send, recv_sem=recv,
            device_id=device, device_id_type=pl.DeviceIdType.MESH,
        )

    def drain(ref, sem):
        pltpu.make_async_copy(ref, ref, sem).wait()

    def weight_copy(i):
        return pltpu.make_async_copy(
            down_ref.at[pl.ds(i * tile, tile)], weights.at[pl.ds(i * tile, tile)],
            weight_sem.at[i],
        )

    dps = [(group + d) % groups for d in range(groups)]
    ers = [(expert + e) % expert_ranks for e in range(expert_ranks)]
    trs = [(tensor + t) % tensor_ranks for t in range(tensor_ranks)]
    peers = [
        (ers[e] * tensor_ranks + trs[t], {"dp": group, "expert": ers[e], "tensor": trs[t]})
        for e in range(expert_ranks) for t in range(tensor_ranks) if e or t
    ]
    others = [
        (
            (dps[d] * expert_ranks + ers[e]) * tensor_ranks + trs[t],
            {"dp": dps[d], "expert": ers[e], "tensor": trs[t]},
        )
        for e in range(expert_ranks) for d in range(groups) for t in range(tensor_ranks)
        if e or d or t
    ]

    barrier = pltpu.get_barrier_semaphore()
    for _, where in others:
        pl.semaphore_signal(
            barrier, inc=1, device_id=where, device_id_type=pl.DeviceIdType.MESH
        )

    loads = [
        pltpu.make_async_copy(ids_hbm, ids_ref, load_sem.at[0]),
        pltpu.make_async_copy(grad_hbm, grad_ref, load_sem.at[1]),
        pltpu.make_async_copy(router_weight_hbm, router_weight_ref, load_sem.at[2]),
        pltpu.make_async_copy(
            router_input_ref.at[pl.ds(pl.multiple_of(tensor * tokens, tokens), tokens)],
            full_input.at[tensor], load_sem.at[3],
        ),
    ]
    for copy in loads:
        copy.start()

    hidden_load = pltpu.make_async_copy(hidden_ref, hidden_rows, hidden_sem)
    hidden_load.start()

    @pl.loop(0, tiles)
    def _(i):
        weight_copy(i).start()

    own_hidden = pltpu.make_async_copy(
        hidden_ref.at[:, pl.ds(pl.multiple_of(group * part, LANES), part)],
        hidden_near.at[0, pl.ds(0, slots)], own_sem,
    )
    own_hidden.start()

    tail = hidden_near.shape[1] - slots
    for buffer in (hidden_near, hidden_far, gated_near, gated_far):
        buffer[:, slots:, :] = jnp.zeros((2, tail, buffer.shape[2]), bf16)
    loads[0].wait()
    labels = iota((experts, tokens), 0)
    pick_first = (ids_ref[0:1, :] == labels).astype(f32)
    pick_second = (ids_ref[1:2, :] == labels).astype(f32)
    pick_both = pick_first + pick_second
    same = (iota((tokens, tokens), 0) == iota((tokens, tokens), 1)).astype(f32)
    first = lax.dot_general(same, pick_first, CONTRACT_LAST, preferred_element_type=f32)
    second = lax.dot_general(same, pick_second, CONTRACT_LAST, preferred_element_type=f32)
    earlier = (iota((tokens, tokens), 1) < iota((tokens, tokens), 0)).astype(f32)
    before = lax.dot_general(pick_both, earlier, CONTRACT_LAST, preferred_element_type=f32)
    spread_rows = ((iota((rows, experts), 0) >> 4) == iota((rows, experts), 1)).astype(f32)
    hit = jnp.dot(spread_rows, pick_both, preferred_element_type=f32)
    rank = jnp.dot(spread_rows, before, preferred_element_type=f32)
    slot = (iota((rows, tokens), 0) & (PAD - 1)).astype(f32)
    table = jnp.where((hit > 0.5) & (jnp.abs(rank - slot) < 0.5), 1.0, 0.0).astype(f32)
    low_table = table.reshape(sources, PAD, tokens)[:, :HALF].reshape(sources * HALF, tokens)
    top_table = jnp.where((pick_both > 0.5) & (jnp.abs(before - HALF) < 0.5), 1.0, 0.0)
    loads[1].wait()
    send_low[...] = (
        jnp.dot(low_table.astype(bf16), grad_ref[...], preferred_element_type=f32)
        .astype(bf16)
        .reshape(send_low.shape)
    )
    send_top[...] = jnp.dot(
        top_table.astype(bf16), grad_ref[...], preferred_element_type=f32
    ).reshape(send_top.shape)

    pl.semaphore_wait(barrier, devices - 1)

    for t in range(1, tensor_ranks):
        remote(
            router_input_ref.at[pl.ds(pl.multiple_of(trs[t] * tokens, tokens), tokens)],
            full_input.at[tensor], input_send, input_recv, {"tensor": trs[t]},
        ).start()
    for to, where in peers:
        remote(send_low.at[to], recv_low.at[source], low_send, low_recv, where).start()
        remote(send_top.at[to], recv_top.at[source], top_send, top_recv, where).start()

    core = group % 2
    half = group // 2
    beside = half * 2 + (1 - core)
    across = (1 - half) * 2 + core
    diagonal = (1 - half) * 2 + (1 - core)
    hidden_to = (
        (beside, hidden_near.at[1, pl.ds(0, slots)], 0),
        (across, hidden_far.at[0, pl.ds(0, slots)], 1),
        (diagonal, hidden_far.at[1, pl.ds(0, slots)], 2),
    )
    hidden_copies = [
        remote(
            hidden_ref.at[:, pl.ds(pl.multiple_of(to * part, LANES), part)], landing,
            hidden_send.at[k], hidden_recv.at[k], {"dp": to},
        )
        for to, landing, k in hidden_to
    ]
    for copy in hidden_copies:
        copy.start()

    recv_top[pl.ds(source, 1)] = send_top[pl.ds(source, 1)]
    recv_low[pl.ds(source, 1)] = send_low[pl.ds(source, 1)]

    height = packed.shape[0]
    column = iota((height, sources * HALF), 1)
    pick_low = (
        iota((height, sources * HALF), 0) == capacity * (column >> 3) + (column & (HALF - 1))
    ).astype(bf16)
    slot_row = iota((height, sources), 0)
    slot_base = capacity * iota((height, sources), 1)
    pick_top = (slot_row == slot_base + HALF).astype(bf16)
    pick_source = ((slot_row >= slot_base) & (slot_row < slot_base + capacity)).astype(f32)
    slot_at = iota((height, LANES), 0) - capacity * jnp.sum(
        pick_source * iota((height, sources), 1).astype(f32), axis=1, keepdims=True
    ).astype(jnp.int32)
    slot_lane = (slot_at == iota((height, LANES), 1)) & (iota((height, LANES), 0) < slots)

    def pull(begin, end):
        for i in range(begin, end):
            weight_copy(i).wait()
        at = slice(begin * tile, end * tile)
        term = jnp.dot(hidden_rows[:, at], weights[at, :], preferred_element_type=f32)
        pulled[...] = pulled[...] + term if begin else term

    cuts = chunk_bounds(tiles)
    early = [c for c in cuts if c[1] <= tiles // 2]
    hidden_load.wait()
    for begin, end in early:
        pull(begin, end)

    loads[2].wait()
    loads[3].wait()
    drain(full_input.at[pl.ds(0, tensor_ranks - 1)], input_recv)
    logits = jnp.zeros((tokens, experts), f32)
    for h in range(tensor_ranks):
        logits = logits + lax.dot_general(
            full_input[h], router_weight_ref[:, h * span : (h + 1) * span], CONTRACT_LAST,
            preferred_element_type=f32,
        )
    chosen = jnp.sum(first * logits, axis=1, keepdims=True)
    rival = jnp.sum(second * logits, axis=1, keepdims=True)
    first_gate = jax.nn.sigmoid(chosen - rival)
    second_gate = jax.nn.sigmoid(rival - chosen)
    gates = first * first_gate + second * second_gate
    low = gates.astype(bf16).astype(f32)
    gate_rows = lax.dot_general(spread_rows, low, CONTRACT_LAST, preferred_element_type=f32)
    slot_gate = jnp.sum(table * gate_rows, axis=1, keepdims=True)
    row_lane = (iota((rows, LANES), 0) & (PAD - 1)) == iota((rows, LANES), 1)
    send_gate[...] = lax.dot_general(
        spread_rows, jnp.where(row_lane, slot_gate, 0.0), CONTRACT_FIRST,
        preferred_element_type=f32,
    ).reshape(send_gate.shape)
    for to, where in peers:
        remote(send_gate.at[to], recv_gate.at[source], gate_send, gate_recv, where).start()
    recv_gate[pl.ds(source, 1)] = send_gate[pl.ds(source, 1)]

    for begin, end in cuts[len(early) :]:
        pull(begin, end)

    drain(recv_low.at[pl.ds(0, sources - 1)], low_recv)
    drain(recv_top.at[pl.ds(0, sources - 1)], top_recv)
    model = packed.shape[1]
    packed[...] = (
        jnp.dot(
            pick_low, recv_low[...].reshape(sources * HALF, model), preferred_element_type=f32
        )
        + jnp.dot(
            pick_top, recv_top[...].reshape(sources, model).astype(bf16),
            preferred_element_type=f32,
        )
    ).astype(bf16)
    partial = jnp.sum(packed[:slots].astype(f32) * pulled[...], axis=1, keepdims=True)
    send_back[...] = lax.dot_general(
        pick_source[:slots], jnp.where(slot_lane[:slots], partial, 0.0), CONTRACT_FIRST,
        precision=EXACT, preferred_element_type=f32,
    ).reshape(send_back.shape)
    for to, where in peers:
        remote(send_back.at[to], recv_back.at[source], back_send, back_recv, where).start()
    recv_back[pl.ds(source, 1)] = send_back[pl.ds(source, 1)]

    drain(recv_gate.at[pl.ds(0, sources - 1)], gate_recv)
    gate_lanes = jnp.dot(
        pick_source, recv_gate[...].reshape(sources, LANES), preferred_element_type=f32
    )
    gate_column = jnp.sum(jnp.where(slot_lane, gate_lanes, 0.0), axis=1, keepdims=True)[:slots]
    gated_near[0, :slots] = (gate_column * packed[:slots].astype(f32)).astype(bf16)

    mine = gated_near.at[0, pl.ds(0, slots)]
    from_beside = gated_near.at[1, pl.ds(0, slots)]
    from_across = gated_far.at[0, pl.ds(0, slots)]
    from_diagonal = gated_far.at[1, pl.ds(0, slots)]
    to_across = remote(mine, from_across, gated_send.at[0], gated_recv.at[0], {"dp": across})
    to_across.start()
    to_beside = remote(mine, from_beside, gated_send.at[1], gated_recv.at[1], {"dp": beside})
    to_beside.start()
    relay = remote(
        from_across, from_diagonal, gated_send.at[2], gated_recv.at[2], {"dp": beside}
    )

    def image_tile(i):
        at = slice(i * tile, (i + 1) * tile)
        image = lax.dot_general(
            weights[at, :], packed[...], CONTRACT_LAST, preferred_element_type=f32
        ).T[:slots]
        hidden_out[:, at] = (gate_column * image).astype(bf16)

    for i in range(tiles // 2):
        image_tile(i)

    drain(recv_back.at[pl.ds(0, sources - 1)], back_recv)
    back_rows = jnp.dot(
        spread_rows, recv_back[...].reshape(sources, LANES), precision=EXACT,
        preferred_element_type=f32,
    )
    returned = jnp.sum(jnp.where(row_lane, back_rows, 0.0), axis=1, keepdims=True)
    gate_grad = lax.dot_general(
        table * returned, spread_rows, CONTRACT_FIRST, precision=EXACT, preferred_element_type=f32
    )
    mixed = jnp.sum(gates * gate_grad, axis=1, keepdims=True)
    logit_grad = gates * (gate_grad - mixed)
    chunk = experts // groups
    block = (span * tensor_ranks) // sources
    terms = split_terms(logit_grad)
    for h in range(tensor_ranks):
        local = lax.dot_general(
            terms, full_input[h], CONTRACT_FIRST, preferred_element_type=f32
        )
        local = local[:experts] + local[experts : 2 * experts] + local[2 * experts :]
        for b in range(span // block):
            x = h * (span // block) + b
            for d in range(groups):
                send_sum[d * sources + x] = local[
                    d * chunk : (d + 1) * chunk, b * block : (b + 1) * block
                ]
    for to, where in others:
        remote(send_sum.at[to], recv_sum.at[me], sum_send, sum_recv, where).start()
    recv_sum[pl.ds(me, 1)] = send_sum[pl.ds(me, 1)]
    input_grad_ref[...] = jnp.dot(
        logit_grad, router_weight_ref[...].astype(f32), precision=EXACT,
        preferred_element_type=f32,
    ).astype(bf16)

    for i in range(tiles // 2, tiles):
        image_tile(i)

    depth = 2 * height
    step = part_tile(part)

    def weight_rows(hidden_pair, gated_pair, i):
        at = slice(i * step, (i + 1) * step)
        return at, lax.dot_general(
            hidden_pair[:, :, at].reshape(depth, step),
            gated_pair[...].reshape(depth, model),
            CONTRACT_FIRST, preferred_element_type=f32,
        )

    own_hidden.wait()
    hidden_copies[0].wait_recv()
    to_beside.wait_recv()
    for i in range(part // step):
        at, term = weight_rows(hidden_near, gated_near, i)
        weight_grad_ref[at, :] = term.astype(bf16)

    to_across.wait_recv()
    relay.start()
    drain(recv_sum.at[pl.ds(0, devices - 1)], sum_recv)
    router_grad_ref[pl.ds(me, 1)] = jnp.sum(recv_sum[...], axis=0, keepdims=True)
    for to, where in others:
        remote(
            router_grad_ref.at[me], router_grad_ref.at[me], whole_send, whole_recv, where
        ).start()

    for copy in hidden_copies[1:]:
        copy.wait_recv()
    relay.wait_recv()
    for i in range(part // step):
        at, term = weight_rows(hidden_far, gated_far, i)
        weight_grad_ref[at, :] = (weight_grad_ref[at, :].astype(f32) + term).astype(bf16)

    for copy in (*hidden_copies, to_across, to_beside, relay):
        copy.wait_send()
    drain(send_low.at[pl.ds(0, sources - 1)], low_send)
    drain(send_top.at[pl.ds(0, sources - 1)], top_send)
    drain(full_input.at[pl.ds(0, tensor_ranks - 1)], input_send)
    drain(send_gate.at[pl.ds(0, sources - 1)], gate_send)
    drain(send_back.at[pl.ds(0, sources - 1)], back_send)
    drain(send_sum.at[pl.ds(0, devices - 1)], sum_send)
    drain(router_grad_ref.at[pl.ds(0, devices - 1)], whole_recv)
    drain(router_grad_ref.at[pl.ds(0, devices - 1)], whole_send)


def split_terms(value):
    parts = []
    for _ in range(3):
        part = value.astype(jnp.bfloat16).astype(jnp.float32)
        parts.append(part)
        value = value - part
    return jnp.concatenate(parts, axis=1).astype(jnp.bfloat16)


def chunk_bounds(tiles):
    bounds, at = [], 0
    while at < tiles:
        size = 3 if tiles - at > 3 else max(1, (tiles - at) // 2 + (tiles - at) % 2)
        bounds.append((at, at + size))
        at += size
    return bounds


def store_kernel(
    sources, weight_ref, hidden_ref, input_ref, router_ref,
    weight_out, hidden_out, input_out, router_out, router_rows, store_sem,
):
    cuts = store_sem.shape[0] - 3
    rows = weight_ref.shape[0] // cuts
    stores = [
        pltpu.make_async_copy(
            weight_ref.at[pl.ds(c * rows, rows)], weight_out.at[pl.ds(c * rows, rows)],
            store_sem.at[c],
        )
        for c in range(cuts)
    ]
    stores.append(pltpu.make_async_copy(hidden_ref, hidden_out, store_sem.at[cuts]))
    stores.append(pltpu.make_async_copy(input_ref, input_out, store_sem.at[cuts + 1]))
    for store in stores:
        store.start()
    pieces, chunk, block = router_ref.shape
    for piece in range(pieces):
        d, x = piece // sources, piece % sources
        router_rows[d * chunk : (d + 1) * chunk, x * block : (x + 1) * block] = router_ref[piece]
    stores.append(pltpu.make_async_copy(router_rows, router_out, store_sem.at[cuts + 2]))
    stores[-1].start()
    for store in stores:
        store.wait()


def by_kernels(router_input, router_weight, expert_ids, down_weight, hidden, grad_output):
    f32, bf16 = jnp.float32, jnp.bfloat16
    tokens, model = grad_output.shape
    experts = router_weight.shape[1]
    groups = lax.axis_size("dp")
    expert_ranks = lax.axis_size("expert")
    tensor_ranks = lax.axis_size("tensor")
    sources = expert_ranks * tensor_ranks
    devices = groups * sources
    slots, width = hidden.shape[1:]
    height = -(-slots // LANES) * LANES
    tile = tile_of(width)
    span = router_input.shape[1]
    part = width // groups
    vmem = pl.BlockSpec(memory_space=pltpu.VMEM)
    hbm = pl.BlockSpec(memory_space=pl.ANY)
    dma = pltpu.SemaphoreType.DMA
    piece = (devices, experts // groups, model // sources)
    weight_grad, hidden_grad, input_grad, router_parts = pl.pallas_call(
        functools.partial(
            exchange_kernel, groups, expert_ranks, tensor_ranks, slots // sources, tile
        ),
        out_shape=(
            OUT((part, model), bf16),
            OUT((slots, width), bf16),
            OUT((tokens, model), bf16),
            OUT(piece, f32),
        ),
        in_specs=[hbm] * 6,
        out_specs=(vmem,) * 4,
        scratch_shapes=[
            pltpu.VMEM((2, tokens), jnp.int32),
            pltpu.VMEM((experts, model), bf16),
            pltpu.VMEM((tokens, model), bf16),
            pltpu.VMEM((tensor_ranks, tokens, span), bf16),
            pltpu.VMEM((width, model), bf16),
            pltpu.VMEM((slots, width), bf16),
            pltpu.VMEM((sources, HALF, model), bf16),
            pltpu.VMEM((sources, HALF, model), bf16),
            pltpu.VMEM((sources, 1, model), f32),
            pltpu.VMEM((sources, 1, model), f32),
            pltpu.VMEM((sources, 1, LANES), f32),
            pltpu.VMEM((sources, 1, LANES), f32),
            pltpu.VMEM((sources, 1, LANES), f32),
            pltpu.VMEM((sources, 1, LANES), f32),
            pltpu.VMEM(piece, f32),
            pltpu.VMEM(piece, f32),
            pltpu.VMEM((height, model), bf16),
            pltpu.VMEM((slots, model), f32),
            pltpu.VMEM((2, height, part), bf16),
            pltpu.VMEM((2, height, model), bf16),
            pltpu.VMEM((2, height, part), bf16),
            pltpu.VMEM((2, height, model), bf16),
            dma((4,)), dma((width // tile,)), dma, dma,
            dma, dma, dma, dma, dma, dma, dma, dma,
            dma((3,)), dma((3,)), dma((3,)), dma((3,)), dma, dma,
            dma, dma, dma, dma,
        ],
        compiler_params=pltpu.CompilerParams(
            collective_id=0, has_side_effects=True, vmem_limit_bytes=VMEM_LIMIT
        ),
        name="exchange",
    )(expert_ids.T, router_weight.T, grad_output, router_input, down_weight, hidden[0])
    weight_grad, hidden_grad, input_grad, router_grad = pl.pallas_call(
        functools.partial(store_kernel, sources),
        out_shape=(
            jax.ShapeDtypeStruct((part, model), bf16),
            jax.ShapeDtypeStruct((slots, width), bf16),
            jax.ShapeDtypeStruct((tokens, model), bf16),
            jax.ShapeDtypeStruct((experts, model), f32),
        ),
        in_specs=[vmem] * 4,
        out_specs=(hbm,) * 4,
        scratch_shapes=[pltpu.VMEM((experts, model), f32), dma((part // part_tile(part) + 3,))],
        compiler_params=pltpu.CompilerParams(vmem_limit_bytes=STORE_LIMIT),
        name="store",
    )(weight_grad, hidden_grad, input_grad, router_parts)
    return weight_grad, hidden_grad[None], router_grad.T, input_grad


def part_tile(part):
    return 384 if part % 384 == 0 else LANES


def tile_of(width):
    for tile in (512, 384, 256):
        if width % tile == 0:
            return tile
    return LANES


def kernels_fit(router_input, router_weight, expert_ids, down_weight, hidden, grad_output):
    groups = lax.axis_size("dp")
    sources = lax.axis_size("expert") * lax.axis_size("tensor")
    slots, width = hidden.shape[1:]
    tokens, model = grad_output.shape
    experts = router_weight.shape[1]
    return (
        groups == 4
        and sources == experts
        and experts % groups == 0
        and slots % 8 == 0
        and slots // sources == HALF + 1
        and slots <= LANES
        and tokens % 16 == 0
        and width % (groups * LANES) == 0
        and model % (sources * LANES) == 0
        and 2 * (width * model + 4 * slots * width + 8 * slots * model) < 48 * 1000 * 1000
    )


def per_device(*arrays):
    return by_kernels(*arrays) if kernels_fit(*arrays) else by_collectives(*arrays)


def by_collectives(router_input, router_weight, expert_ids, down_weight, hidden, grad_output):
    token_rows = grad_output.shape[0]
    model_width = grad_output.shape[1]
    expert_count = router_weight.shape[1]
    choose_count = expert_ids.shape[1]
    expert_ranks = lax.axis_size("expert")
    tensor_ranks = lax.axis_size("tensor")
    sources = expert_ranks * tensor_ranks
    spread = sources // expert_count
    capacity = hidden.shape[1] // sources
    full_input = lax.all_to_all(router_input, "tensor", split_axis=0, concat_axis=1, tiled=True)
    logits = jnp.dot(full_input, router_weight, preferred_element_type=jnp.float32)
    labels = jnp.arange(expert_count, dtype=jnp.int32)
    onehot_int = (expert_ids[:, :, None] == labels).astype(jnp.int32)
    onehot = onehot_int.astype(jnp.float32)
    picked = jnp.sum(onehot * logits[:, None, :], axis=2)
    first_gate = jax.nn.sigmoid(picked[:, 0] - picked[:, 1])
    second_gate = jax.nn.sigmoid(picked[:, 1] - picked[:, 0])
    gate_values = jnp.stack([first_gate, second_gate], axis=1)
    gate_low = gate_values.astype(jnp.bfloat16)
    flat_hits = onehot_int.reshape(token_rows * choose_count, expert_count)
    before = jnp.cumsum(flat_hits, axis=0) - flat_hits
    slot_pos = jnp.sum(before * flat_hits, axis=1).reshape(token_rows, choose_count)
    slot_ids = jnp.arange(capacity, dtype=jnp.int32)
    dispatch_table = onehot[:, :, :, None] * (slot_pos[:, :, None, None] == slot_ids).astype(
        jnp.float32
    )
    slot_table = jnp.sum(dispatch_table, axis=1).astype(jnp.bfloat16)
    packed_grad = jnp.einsum(
        "rec,rd->ecd", slot_table, grad_output, preferred_element_type=jnp.float32
    ).astype(jnp.bfloat16)
    packed_gate = jnp.einsum("rkec,rk->ec", dispatch_table, gate_low.astype(jnp.float32)).astype(
        jnp.bfloat16
    )
    send_grad = jnp.repeat(packed_grad, spread, axis=0)
    send_gate = jnp.repeat(packed_gate, spread, axis=0)
    recv_grad, recv_gate = (
        lax.all_to_all(send_grad, ("expert", "tensor"), split_axis=0, concat_axis=0, tiled=True),
        lax.all_to_all(send_gate, ("expert", "tensor"), split_axis=0, concat_axis=0, tiled=True),
    )
    recv_grad = recv_grad.reshape(sources * capacity, model_width)
    recv_gate = recv_gate.reshape(sources * capacity).astype(jnp.float32)
    hidden_rows = hidden[0]
    gated_grad = (recv_gate[:, None] * recv_grad.astype(jnp.float32)).astype(jnp.bfloat16)
    expert_image = lax.dot_general(
        recv_grad, down_weight, (((1,), (1,)), ((), ())), preferred_element_type=jnp.float32
    )
    hidden_part = (recv_gate[:, None] * expert_image).astype(jnp.bfloat16)
    gate_partial = jnp.sum(hidden_rows.astype(jnp.float32) * expert_image, axis=1).reshape(
        sources, capacity
    )
    returned = lax.all_to_all(
        gate_partial, ("expert", "tensor"), split_axis=0, concat_axis=0, tiled=True
    )
    expert_sums = jnp.sum(returned.reshape(expert_count, spread, capacity), axis=1)
    gate_grad = jnp.einsum("rkec,ec->rk", dispatch_table, expert_sums)
    mixed_term = jnp.sum(gate_values * gate_grad, axis=1, keepdims=True)
    logit_part = gate_values * (gate_grad - mixed_term)
    logit_grad = jnp.sum(onehot * logit_part[:, :, None], axis=1)
    input_grad = jnp.dot(
        logit_grad, router_weight.astype(jnp.float32).T, precision=lax.Precision.HIGHEST
    ).astype(jnp.bfloat16)
    router_local = jnp.dot(
        full_input.astype(jnp.float32).T, logit_grad, precision=lax.Precision.HIGHEST
    )
    router_grad = lax.psum(router_local, ("dp", "expert", "tensor"))
    hidden_all = lax.all_to_all(hidden_rows, "dp", split_axis=1, concat_axis=0, tiled=True)
    gated_all = lax.all_gather(gated_grad, "dp", axis=0, tiled=True)
    weight_sum = lax.dot_general(
        hidden_all, gated_all, (((0,), (0,)), ((), ())), preferred_element_type=jnp.float32
    ).astype(jnp.bfloat16)
    return (weight_sum, hidden_part[None], router_grad, input_grad)


def solution(mesh):
    return jax.shard_map(
        per_device,
        mesh=mesh,
        in_specs=(
            P(("dp", "expert"), "tensor"),
            P(),
            P(("dp", "expert", "tensor"), None),
            P(("expert", "tensor"), None),
            P("dp", None, ("expert", "tensor")),
            P(("dp", "expert", "tensor"), None),
        ),
        out_specs=(
            P(("expert", "tensor", "dp"), None),
            P("dp", None, ("expert", "tensor")),
            P(),
            P(("dp", "expert", "tensor"), None),
        ),
        check_vma=False,
    )
```

time: 62.9 us -> 40.1 us (0.64)
  Pallas kernels: 62 us -> 39.1 us
    pallas_call x1, Pallas kernels: 53 us -> 35.5 us  [by_kernels(): pl.pallas_call(functools.partial(exchange_kernel, groups, expert_ranks, t...]
    pallas_call x1, Pallas kernels: 9 us -> 3.57 us  [by_kernels(): pl.pallas_call(functools.partial(store_kernel, sources), out_shape=(jax.S...]
where the time goes in v1:
time: 40.1 us; the launch traced here: 39.9 us
  Pallas kernels  39.1 us (98%)
  between operations  0.8 us (2%)
    pallas_call x1, Pallas kernels, by_kernels(): pl.pallas_call(functools.partial(exchange_kernel, groups, expert_ranks, t...  35.5 us
    pallas_call x1, Pallas kernels, by_kernels(): pl.pallas_call(functools.partial(store_kernel, sources), out_shape=(jax.S...  3.57 us

profile of v1, /device:TPU:0, one launch (start us, length us, event | category | flops | bytes accessed | tf_op | source)
XLA Modules:
  0.0 39.9 jit_solution(2765723582435557909)
XLA Ops:
  0.6 35.5 %exchange.1 = (bf16[1920,2048]{1,0:T(8,128)(2,1)S(1)}, bf16[72,7680]{1,0:T(8,128)(2,1)S(1)}, bf16[32,2048]{1,0:T(8,128)(2,1)S(1)}, f32[32,2,256]{2,1,0:T(2,128)S(1)}) custom-call(s32[2,32]{1,0:T(2,128)} %bitcast.7, bf16[8,2048]{1,0:T(8,128)(2,1)} %bitcast.6, bf16[32,2048]{1,0:T(8,128)(2,1)} %grad_hbm.1, bf16[64,1024]{1,0:T(8,128)(2,1)} %router_input_ref.1, ...), custom_call_target="tpu_custom_call" | custom-call | tf_op jit(solution)/shard_map/exchange/pallas_call | solution.py:431
  36.2 3.6 %store.1 = (bf16[1920,2048]{1,0:T(8,128)(2,1)}, bf16[72,7680]{1,0:T(8,128)(2,1)}, bf16[32,2048]{1,0:T(8,128)(2,1)}, f32[8,2048]{1,0:T(8,128)}) custom-call(bf16[1920,2048]{1,0:T(8,128)(2,1)S(1)} %get-tuple-element.12.weight_ref, bf16[72,7680]{1,0:T(8,128)(2,1)S(1)} %get-tuple-element.13.hidden_ref, bf16[32,2048]{1,0:T(8,128)(2,1)S(1)} %get-tuple-element.14.input_ref, ...), custom_call_target="tpu_custom_call" | custom-call | tf_op jit(solution)/shard_map/store/pallas_call | solution.py:476

commit v2 on v1

v2 whole, which is shorter than its diff:
```python
import functools

import jax
import jax.numpy as jnp
from jax import lax
from jax.experimental import pallas as pl
from jax.experimental.pallas import tpu as pltpu
from jax.sharding import PartitionSpec as P


PAD = 16
LANES = 128
HALF = 8
VMEM_LIMIT = 50 * 1000 * 1000
WEIGHT_LIMIT = 24 * 1000 * 1000
OUT = pltpu.VMEM
PAUSE = 8
LAST_TILES = 2
EXACT = lax.Precision.HIGHEST
CONTRACT_LAST = (((1,), (1,)), ((), ()))
CONTRACT_FIRST = (((0,), (0,)), ((), ()))


def iota(shape, axis):
    return lax.broadcasted_iota(jnp.int32, shape, axis)


def exchange_kernel(
    groups, expert_ranks, tensor_ranks, capacity, tile,
    ids_hbm, router_weight_hbm, grad_hbm, router_input_ref, down_ref, hidden_ref,
    near_ref, hidden_near, gated_near, hidden_far, gated_far, hidden_out, input_grad_ref,
    router_grad_ref, ids_ref, router_weight_ref, grad_ref, own_input, weights, hidden_rows,
    send_low, recv_low, send_top, recv_top, send_back, recv_back,
    send_info, recv_info, column_input, slot_weight, slot_sign, logit_rows, group_sums,
    send_logit, recv_logit, packed, pulled,
    load_sem, weight_sem, hidden_sem, own_sem,
    logit_send, logit_recv, low_send, low_recv, top_send, top_recv,
    hidden_send, hidden_recv, gated_send, gated_recv, back_send, back_recv,
    info_send, info_recv, column_send, column_recv, sum_send, sum_recv, whole_send, whole_recv,
):
    f32, bf16 = jnp.float32, jnp.bfloat16
    group = lax.axis_index("dp")
    expert = lax.axis_index("expert")
    tensor = lax.axis_index("tensor")
    sources = expert_ranks * tensor_ranks
    source = expert * tensor_ranks + tensor
    slots, width = hidden_ref.shape
    part = width // groups
    experts = router_weight_ref.shape[0]
    tokens = grad_ref.shape[0]
    span = router_input_ref.shape[1]
    feats = span // expert_ranks
    rows = sources * PAD
    tiles = width // tile

    def remote(src, dst, send, recv, device):
        return pltpu.make_async_remote_copy(
            src_ref=src, dst_ref=dst, send_sem=send, recv_sem=recv,
            device_id=device, device_id_type=pl.DeviceIdType.MESH,
        )

    def drain(ref, sem):
        pltpu.make_async_copy(ref, ref, sem).wait()

    cuts = chunk_bounds(tiles)
    weight_copies = [
        pltpu.make_async_copy(
            down_ref.at[pl.ds(begin * tile, (end - begin) * tile)],
            weights.at[pl.ds(begin * tile, (end - begin) * tile)], weight_sem.at[c],
        )
        for c, (begin, end) in enumerate(cuts)
    ]

    ers = [(expert + e) % expert_ranks for e in range(expert_ranks)]
    trs = [(tensor + t) % tensor_ranks for t in range(tensor_ranks)]
    peers = [
        (ers[e] * tensor_ranks + trs[t], {"dp": group, "expert": ers[e], "tensor": trs[t]})
        for e in range(expert_ranks) for t in range(tensor_ranks) if e or t
    ]
    core = group % 2
    half = group // 2
    beside = half * 2 + (1 - core)
    across = (1 - half) * 2 + core
    diagonal = (1 - half) * 2 + (1 - core)
    mates = [
        {"dp": to, "expert": expert, "tensor": tensor} for to in (across, diagonal, beside)
    ]

    loads = [
        pltpu.make_async_copy(ids_hbm, ids_ref, load_sem.at[0]),
        pltpu.make_async_copy(grad_hbm, grad_ref, load_sem.at[1]),
        pltpu.make_async_copy(router_weight_hbm, router_weight_ref, load_sem.at[2]),
        pltpu.make_async_copy(router_input_ref, own_input, load_sem.at[3]),
        pltpu.make_async_copy(
            router_input_ref.at[:, pl.ds(pl.multiple_of(expert * feats, LANES), feats)],
            column_input.at[expert], load_sem.at[4],
        ),
    ]
    for copy in loads:
        copy.start()

    hidden_load = pltpu.make_async_copy(hidden_ref, hidden_rows, hidden_sem)
    hidden_load.start()

    for copy in weight_copies:
        copy.start(priority=1)
    own_hidden = pltpu.make_async_copy(
        hidden_ref.at[:, pl.ds(pl.multiple_of(group * part, LANES), part)],
        hidden_near.at[0, pl.ds(0, slots)], own_sem,
    )
    own_hidden.start()

    barrier = pltpu.get_barrier_semaphore()
    for where in [place for _, place in peers] + mates:
        pl.semaphore_signal(
            barrier, inc=1, device_id=where, device_id_type=pl.DeviceIdType.MESH
        )

    send_info[...] = jnp.zeros_like(send_info)
    tail = hidden_near.shape[1] - slots
    for buffer in (hidden_near, hidden_far, gated_near, gated_far):
        buffer[:, slots:, :] = jnp.zeros((2, tail, buffer.shape[2]), bf16)
    loads[0].wait()
    labels = iota((experts, tokens), 0)
    pick_first = (ids_ref[0:1, :] == labels).astype(f32)
    pick_second = (ids_ref[1:2, :] == labels).astype(f32)
    pick_both = pick_first + pick_second
    earlier = (iota((tokens, tokens), 1) < iota((tokens, tokens), 0)).astype(f32)
    before = lax.dot_general(pick_both, earlier, CONTRACT_LAST, preferred_element_type=f32)
    spread_rows = ((iota((rows, experts), 0) >> 4) == iota((rows, experts), 1)).astype(f32)
    hit = jnp.dot(spread_rows, pick_both, preferred_element_type=f32)
    rank = jnp.dot(spread_rows, before, preferred_element_type=f32)
    slot = (iota((rows, tokens), 0) & (PAD - 1)).astype(f32)
    table = jnp.where((hit > 0.5) & (jnp.abs(rank - slot) < 0.5), 1.0, 0.0).astype(f32)
    low_table = table.reshape(sources, PAD, tokens)[:, :HALF].reshape(sources * HALF, tokens)
    top_table = jnp.where((pick_both > 0.5) & (jnp.abs(before - HALF) < 0.5), 1.0, 0.0)
    loads[1].wait()
    wide = send_low.shape[3]
    for h in range(2):
        send_low[h] = (
            jnp.dot(
                low_table.astype(bf16), grad_ref[:, h * wide : (h + 1) * wide],
                preferred_element_type=f32,
            )
            .astype(bf16)
            .reshape(send_low.shape[1:])
        )
    send_top[...] = jnp.dot(
        top_table.astype(bf16), grad_ref[...], preferred_element_type=f32
    ).reshape(send_top.shape)

    loads[2].wait()
    loads[3].wait()
    own_weight = router_weight_ref[:, pl.ds(pl.multiple_of(tensor * span, LANES), span)]

    def part_logits(t):
        return lax.dot_general(
            own_weight, own_input[pl.ds(pl.multiple_of(trs[t] * tokens, tokens), tokens)],
            CONTRACT_LAST, preferred_element_type=f32,
        )

    for t in range(1, tensor_ranks):
        send_logit[t] = part_logits(t)
    send_logit[0] = part_logits(0)

    pl.semaphore_wait(barrier, len(peers) + len(mates))

    for t in range(1, tensor_ranks):
        remote(
            send_logit.at[t], recv_logit.at[t], logit_send, logit_recv, {"tensor": trs[t]}
        ).start()
    for to, where in peers:
        remote(
            send_low.at[0, to], recv_low.at[0, source], low_send, low_recv.at[0], where
        ).start()
    for to, where in peers:
        remote(
            send_low.at[1, to], recv_low.at[1, source], low_send, low_recv.at[1], where
        ).start()
        remote(send_top.at[to], recv_top.at[source], top_send, top_recv, where).start()

    hidden_to = (
        (beside, hidden_near.at[1, pl.ds(0, slots)], 0),
        (across, hidden_far.at[0, pl.ds(0, slots)], 1),
        (diagonal, hidden_far.at[1, pl.ds(0, slots)], 2),
    )
    hidden_copies = [
        remote(
            hidden_rows.at[:, pl.ds(pl.multiple_of(to * part, LANES), part)], landing,
            hidden_send.at[k], hidden_recv.at[k], {"dp": to},
        )
        for to, landing, k in hidden_to
    ]
    hidden_load.wait()
    for copy in hidden_copies:
        copy.start()

    recv_top[pl.ds(source, 1)] = send_top[pl.ds(source, 1)]
    for h in range(2):
        recv_low[h, pl.ds(source, 1)] = send_low[h, pl.ds(source, 1)]

    height = packed.shape[0]
    column = iota((height, sources * HALF), 1)
    pick_low = (
        iota((height, sources * HALF), 0) == capacity * (column >> 3) + (column & (HALF - 1))
    ).astype(bf16)
    slot_row = iota((height, sources), 0)
    slot_base = capacity * iota((height, sources), 1)
    pick_top = (slot_row == slot_base + HALF).astype(bf16)
    pick_source = ((slot_row >= slot_base) & (slot_row < slot_base + capacity)).astype(f32)
    slot_at = iota((height, LANES), 0) - capacity * jnp.sum(
        pick_source * iota((height, sources), 1).astype(f32), axis=1, keepdims=True
    ).astype(jnp.int32)
    slot_lane = (slot_at == iota((height, LANES), 1)) & (iota((height, LANES), 0) < slots)

    def pull(c):
        begin, end = cuts[c]
        weight_copies[c].wait()
        at = slice(begin * tile, end * tile)
        term = jnp.dot(hidden_rows[:, at], weights[at, :], preferred_element_type=f32)
        pulled[...] = pulled[...] + term if c else term

    early = 1
    for c in range(early):
        pull(c)

    drain(recv_logit.at[pl.ds(0, tensor_ranks - 1)], logit_recv)
    logits = send_logit[0]
    for t in range(1, tensor_ranks):
        logits = logits + recv_logit[t]
    chosen = jnp.sum(pick_first * logits, axis=0, keepdims=True)
    rival = jnp.sum(pick_second * logits, axis=0, keepdims=True)
    first_gate = jax.nn.sigmoid(chosen - rival)
    second_gate = jax.nn.sigmoid(rival - chosen)
    numbered = before + PAD * labels.astype(f32)
    send_info[0:1, :tokens] = jnp.sum(pick_first * numbered, axis=0, keepdims=True)
    send_info[1:2, :tokens] = jnp.sum(pick_second * numbered, axis=0, keepdims=True)
    send_info[2:3, :tokens] = first_gate * second_gate
    send_info[3:4, :tokens] = first_gate.astype(bf16).astype(f32)
    send_info[4:5, :tokens] = second_gate.astype(bf16).astype(f32)
    for _, where in peers:
        remote(send_info, recv_info.at[source], info_send, info_recv, where).start()
    recv_info[pl.ds(source, 1)] = send_info[...][None]

    for c in range(early, len(cuts)):
        pull(c)

    drain(recv_info.at[pl.ds(0, sources - 1)], info_recv)
    for h in range(2):
        drain(recv_low.at[h, pl.ds(0, sources - 1)], low_recv.at[h])
    drain(recv_top.at[pl.ds(0, sources - 1)], top_recv)
    model = packed.shape[1]
    for h in range(2):
        at = slice(h * wide, (h + 1) * wide)
        packed[:, at] = (
            jnp.dot(
                pick_low, recv_low[h].reshape(sources * HALF, wide), preferred_element_type=f32
            )
            + jnp.dot(
                pick_top, recv_top[:, :, at].reshape(sources, wide).astype(bf16),
                preferred_element_type=f32,
            )
        ).astype(bf16)
    partial = jnp.sum(packed[:slots].astype(f32) * pulled[...], axis=1, keepdims=True)
    own_lane = (iota((slots, LANES), 1) - PAD * source) == slot_at[:slots]
    send_back[...] = lax.dot_general(
        pick_source[:slots], jnp.where(own_lane, partial, 0.0), CONTRACT_FIRST,
        precision=EXACT, preferred_element_type=f32,
    )
    for _, where in peers:
        remote(send_back, recv_back.at[source], back_send, back_recv, where).start()
    for e in range(1, expert_ranks):
        remote(
            own_input.at[:, pl.ds(pl.multiple_of(ers[e] * feats, LANES), feats)],
            column_input.at[expert], column_send, column_recv, {"expert": ers[e]},
        ).start()
    recv_back[pl.ds(source, 1)] = send_back[...][None]

    known = recv_info[...].reshape(sources * HALF, LANES)
    known = jnp.concatenate([known, jnp.zeros((LANES - sources * HALF, LANES), f32)], axis=0).T
    slot_lanes = iota((tokens, LANES), 1).astype(f32)
    label_lanes = PAD * iota((tokens, experts), 1).astype(f32)
    gate_lanes = jnp.zeros((height, LANES), f32)
    for x in range(sources):
        one, two, share, one_gate, two_gate = (
            known[:tokens, x * HALF + k : x * HALF + k + 1] for k in range(5)
        )
        slot_weight[x] = jnp.where(
            slot_lanes == one, share, jnp.where(slot_lanes == two, -share, 0.0)
        )
        slot_sign[x] = jnp.where(
            (one >= label_lanes) & (one < label_lanes + PAD), 1.0, 0.0
        ) - jnp.where((two >= label_lanes) & (two < label_lanes + PAD), 1.0, 0.0)
        gate_row = jnp.sum(
            jnp.where(
                slot_lanes == one, one_gate, jnp.where(slot_lanes == two, two_gate, 0.0)
            ),
            axis=0, keepdims=True,
        )
        gate_lanes = gate_lanes + pick_source[:, x : x + 1] * gate_row
    gate_column = jnp.sum(
        jnp.where(own_lane, gate_lanes[:slots], 0.0), axis=1, keepdims=True
    )
    gated_near[0, :slots] = (gate_column * packed[:slots].astype(f32)).astype(bf16)

    fold = model * 3 // 8 // LANES * LANES
    spans = (pl.ds(0, fold), pl.ds(fold, model - fold))

    def gated_part(buffer, k, h):
        return buffer.at[k, pl.ds(0, slots), spans[h]]

    to_across, to_beside, relays = [], [], []
    for h in range(2):
        mine = gated_part(gated_near, 0, h)
        from_beside = gated_part(gated_near, 1, h)
        from_across = gated_part(gated_far, 0, h)
        from_diagonal = gated_part(gated_far, 1, h)
        to_across.append(
            remote(mine, from_across, gated_send.at[0, h], gated_recv.at[0, h], {"dp": across})
        )
        to_beside.append(
            remote(mine, from_beside, gated_send.at[1, h], gated_recv.at[1, h], {"dp": beside})
        )
        relays.append(
            remote(
                from_across, from_diagonal, gated_send.at[2, h], gated_recv.at[2, h],
                {"dp": beside},
            )
        )
    to_across[0].start()
    for copy in to_beside:
        copy.start()

    def image_tile(i):
        at = slice(i * tile, (i + 1) * tile)
        image = lax.dot_general(
            weights[at, :], packed[...], CONTRACT_LAST, preferred_element_type=f32
        ).T[:slots]
        hidden_out[:, at] = (gate_column * image).astype(bf16)

    pause = tiles * PAUSE // 15
    for i in range(pause):
        image_tile(i)

    drain(recv_back.at[pl.ds(0, sources - 1)], back_recv)
    returned = recv_back[0]
    for e in range(1, experts):
        returned = returned + recv_back[e]
    for x in range(sources):
        logit_rows[x] = slot_sign[x] * jnp.sum(
            slot_weight[x] * returned[x : x + 1], axis=1, keepdims=True
        )
    terms = split_terms(logit_rows[...].reshape(sources * tokens, experts))
    loads[4].wait()
    drain(column_input.at[pl.ds(0, expert_ranks - 1)], column_recv)
    sums = lax.dot_general(
        terms, column_input[...].reshape(sources * tokens, feats), CONTRACT_FIRST,
        preferred_element_type=f32,
    )
    group_sums[pl.ds(group, 1)] = (
        sums[:experts] + sums[experts : 2 * experts] + sums[2 * experts :]
    )[None]
    for where in mates:
        remote(
            group_sums.at[group], group_sums.at[group], sum_send, sum_recv, where
        ).start()
    to_across[1].start()
    input_grad_ref[...] = jnp.dot(
        logit_rows[pl.ds(source, 1)].reshape(tokens, experts),
        router_weight_ref[...].astype(f32), precision=EXACT,
        preferred_element_type=f32,
    ).astype(bf16)

    later = max(pause, tiles - LAST_TILES)
    for i in range(pause, later):
        image_tile(i)

    to_across[0].wait_recv()
    relays[0].start()
    drain(group_sums.at[pl.ds(0, groups - 1)], sum_recv)
    total = group_sums[0]
    for d in range(1, groups):
        total = total + group_sums[d]
    router_grad_ref[pl.ds(source, 1)] = total[None]
    for _, where in peers:
        remote(
            router_grad_ref.at[source], router_grad_ref.at[source], whole_send, whole_recv, where
        ).start()
    for i in range(later, tiles):
        image_tile(i)


    step = part_tile(part)

    to_across[1].wait_recv()
    relays[1].start()
    own_hidden.wait()
    hidden_copies[0].wait_recv()
    for copy in to_beside:
        copy.wait_recv()
    for i in range(near_ref.shape[0] // step):
        at = slice(i * step, (i + 1) * step)
        near_ref[at, :] = pair_product(hidden_near, gated_near, at).astype(bf16)

    for copy in hidden_copies[1:]:
        copy.wait_recv()
    for copy in relays:
        copy.wait_recv()
    for copy in (*hidden_copies, *to_across, *to_beside, *relays):
        copy.wait_send()
    drain(send_low.at[:, pl.ds(0, sources - 1)], low_send)
    drain(send_top.at[pl.ds(0, sources - 1)], top_send)
    drain(recv_logit.at[pl.ds(0, tensor_ranks - 1)], logit_send)
    drain(recv_back.at[pl.ds(0, sources - 1)], back_send)
    drain(recv_info.at[pl.ds(0, sources - 1)], info_send)
    drain(column_input.at[pl.ds(0, expert_ranks - 1)], column_send)
    drain(group_sums.at[pl.ds(0, groups - 1)], sum_send)
    drain(router_grad_ref.at[pl.ds(0, sources - 1)], whole_recv)
    drain(router_grad_ref.at[pl.ds(0, sources - 1)], whole_send)


def split_terms(value):
    parts = []
    for _ in range(3):
        part = value.astype(jnp.bfloat16).astype(jnp.float32)
        parts.append(part)
        value = value - part
    return jnp.concatenate(parts, axis=1).astype(jnp.bfloat16)


def chunk_bounds(tiles):
    bounds, at = [], 0
    while at < tiles:
        size = 3 if tiles - at > 3 else max(1, (tiles - at) // 2 + (tiles - at) % 2)
        bounds.append((at, at + size))
        at += size
    return bounds


def pair_product(hidden_ref, gated_ref, at):
    depth = hidden_ref.shape[0] * hidden_ref.shape[1]
    return lax.dot_general(
        hidden_ref[:, :, at].reshape(depth, at.stop - at.start),
        gated_ref[...].reshape(depth, gated_ref.shape[2]),
        CONTRACT_FIRST, preferred_element_type=jnp.float32,
    )


def weight_kernel(
    tensor_ranks, near_ref, hidden_near, gated_near, hidden_far, gated_far, hidden_ref, input_ref, router_ref,
    weight_out, hidden_out, input_out, router_out, weight_rows, router_rows, store_sem,
):
    bounds = row_bounds(weight_rows.shape[0])
    ready = near_ref.shape[0]
    cuts = len(bounds)
    stores = [
        pltpu.make_async_copy(hidden_ref, hidden_out, store_sem.at[cuts]),
        pltpu.make_async_copy(input_ref, input_out, store_sem.at[cuts + 1]),
    ]
    for store in stores:
        store.start()
    for c, (begin, end) in enumerate(bounds):
        at = slice(begin, end)
        far = pair_product(hidden_far, gated_far, at)
        if end <= ready:
            near = near_ref[at, :].astype(jnp.float32)
        else:
            near = pair_product(hidden_near, gated_near, at)
        weight_rows[at, :] = (far + near).astype(weight_rows.dtype)
        rows = pl.ds(begin, end - begin)
        stores.append(
            pltpu.make_async_copy(weight_rows.at[rows], weight_out.at[rows], store_sem.at[c])
        )
        stores[-1].start()
    sources, _, feats = router_ref.shape
    for x in range(sources):
        e, t = x // tensor_ranks, x % tensor_ranks
        column = (t * (sources // tensor_ranks) + e) * feats
        router_rows[:, column : column + feats] = router_ref[x]
    stores.append(pltpu.make_async_copy(router_rows, router_out, store_sem.at[cuts + 2]))
    stores[-1].start()
    for store in stores:
        store.wait()


def by_kernels(router_input, router_weight, expert_ids, down_weight, hidden, grad_output):
    f32, bf16 = jnp.float32, jnp.bfloat16
    tokens, model = grad_output.shape
    experts = router_weight.shape[1]
    groups = lax.axis_size("dp")
    expert_ranks = lax.axis_size("expert")
    tensor_ranks = lax.axis_size("tensor")
    sources = expert_ranks * tensor_ranks
    slots, width = hidden.shape[1:]
    height = -(-slots // LANES) * LANES
    tile = tile_of(width)
    span = router_input.shape[1]
    part = width // groups
    vmem = pl.BlockSpec(memory_space=pltpu.VMEM)
    hbm = pl.BlockSpec(memory_space=pl.ANY)
    dma = pltpu.SemaphoreType.DMA
    feats = span // expert_ranks
    near, *pairs, hidden_grad, input_grad, router_parts = pl.pallas_call(
        functools.partial(
            exchange_kernel, groups, expert_ranks, tensor_ranks, slots // sources, tile
        ),
        out_shape=(
            OUT((near_rows(part), model), bf16),
            OUT((2, height, part), bf16),
            OUT((2, height, model), bf16),
            OUT((2, height, part), bf16),
            OUT((2, height, model), bf16),
            OUT((slots, width), bf16),
            OUT((tokens, model), bf16),
            OUT((sources, experts, feats), f32),
        ),
        in_specs=[hbm] * 6,
        out_specs=(vmem,) * 8,
        scratch_shapes=[
            pltpu.VMEM((2, tokens), jnp.int32),
            pltpu.VMEM((experts, model), bf16),
            pltpu.VMEM((tokens, model), bf16),
            pltpu.VMEM((tensor_ranks * tokens, span), bf16),
            pltpu.VMEM((width, model), bf16),
            pltpu.VMEM((slots, width), bf16),
            pltpu.VMEM((2, sources, HALF, model // 2), bf16),
            pltpu.VMEM((2, sources, HALF, model // 2), bf16),
            pltpu.VMEM((sources, 1, model), f32),
            pltpu.VMEM((sources, 1, model), f32),
            pltpu.VMEM((sources, LANES), f32),
            pltpu.VMEM((experts, sources, LANES), f32),
            pltpu.VMEM((HALF, LANES), f32),
            pltpu.VMEM((sources, HALF, LANES), f32),
            pltpu.VMEM((expert_ranks, tensor_ranks * tokens, feats), bf16),
            pltpu.VMEM((sources, tokens, LANES), f32),
            pltpu.VMEM((sources, tokens, experts), f32),
            pltpu.VMEM((sources, tokens, experts), f32),
            pltpu.VMEM((groups, experts, feats), f32),
            pltpu.VMEM((tensor_ranks, experts, tokens), f32),
            pltpu.VMEM((tensor_ranks, experts, tokens), f32),
            pltpu.VMEM((height, model), bf16),
            pltpu.VMEM((slots, model), f32),
            dma((5,)), dma((len(chunk_bounds(width // tile)),)), dma, dma,
            dma, dma, dma, dma((2,)), dma, dma,
            dma((3,)), dma((3,)), dma((3, 2)), dma((3, 2)), dma, dma,
            dma, dma, dma, dma, dma, dma, dma, dma,
        ],
        compiler_params=pltpu.CompilerParams(
            collective_id=0, has_side_effects=True, vmem_limit_bytes=VMEM_LIMIT
        ),
        name="exchange",
    )(expert_ids.T, router_weight.T, grad_output, router_input, down_weight, hidden[0])
    weight_grad, hidden_grad, input_grad, router_grad = pl.pallas_call(
        functools.partial(weight_kernel, tensor_ranks),
        out_shape=(
            jax.ShapeDtypeStruct((part, model), bf16),
            jax.ShapeDtypeStruct((slots, width), bf16),
            jax.ShapeDtypeStruct((tokens, model), bf16),
            jax.ShapeDtypeStruct((experts, model), f32),
        ),
        in_specs=[vmem] * 8,
        out_specs=(hbm,) * 4,
        scratch_shapes=[
            pltpu.VMEM((part, model), bf16),
            pltpu.VMEM((experts, model), f32),
            dma((len(row_bounds(part)) + 3,)),
        ],
        compiler_params=pltpu.CompilerParams(vmem_limit_bytes=WEIGHT_LIMIT),
        name="weight_grad",
    )(near, *pairs, hidden_grad, input_grad, router_parts)
    return weight_grad, hidden_grad[None], router_grad.T, input_grad


def near_rows(part):
    step = part_tile(part)
    return part // step * 3 // 5 * step


def row_bounds(part):
    units, ready, bounds, at = part // LANES, near_rows(part) // LANES, [], 0
    while at < units:
        stop = ready if at < ready else units
        size = min(stop - at, 2 if at == 0 or at >= ready else 3)
        bounds.append((at * LANES, (at + size) * LANES))
        at += size
    return bounds


def part_tile(part):
    return 384 if part % 384 == 0 else LANES


def tile_of(width):
    for tile in (512, 384, 256):
        if width % tile == 0:
            return tile
    return LANES


def kernels_fit(router_input, router_weight, expert_ids, down_weight, hidden, grad_output):
    groups = lax.axis_size("dp")
    sources = lax.axis_size("expert") * lax.axis_size("tensor")
    slots, width = hidden.shape[1:]
    tokens, model = grad_output.shape
    experts = router_weight.shape[1]
    return (
        groups == 4
        and sources == experts
        and slots % 8 == 0
        and slots // sources == HALF + 1
        and slots <= LANES
        and tokens % 16 == 0
        and width % (groups * LANES) == 0
        and router_input.shape[1] % (lax.axis_size("expert") * LANES) == 0
        and sources * PAD <= LANES
        and 2 * (width * model + 4 * slots * width + 8 * slots * model) < 48 * 1000 * 1000
    )


def per_device(*arrays):
    return by_kernels(*arrays) if kernels_fit(*arrays) else by_collectives(*arrays)


def by_collectives(router_input, router_weight, expert_ids, down_weight, hidden, grad_output):
    token_rows = grad_output.shape[0]
    model_width = grad_output.shape[1]
    expert_count = router_weight.shape[1]
    choose_count = expert_ids.shape[1]
    expert_ranks = lax.axis_size("expert")
    tensor_ranks = lax.axis_size("tensor")
    sources = expert_ranks * tensor_ranks
    spread = sources // expert_count
    capacity = hidden.shape[1] // sources
    full_input = lax.all_to_all(router_input, "tensor", split_axis=0, concat_axis=1, tiled=True)
    logits = jnp.dot(full_input, router_weight, preferred_element_type=jnp.float32)
    labels = jnp.arange(expert_count, dtype=jnp.int32)
    onehot_int = (expert_ids[:, :, None] == labels).astype(jnp.int32)
    onehot = onehot_int.astype(jnp.float32)
    picked = jnp.sum(onehot * logits[:, None, :], axis=2)
    first_gate = jax.nn.sigmoid(picked[:, 0] - picked[:, 1])
    second_gate = jax.nn.sigmoid(picked[:, 1] - picked[:, 0])
    gate_values = jnp.stack([first_gate, second_gate], axis=1)
    gate_low = gate_values.astype(jnp.bfloat16)
    flat_hits = onehot_int.reshape(token_rows * choose_count, expert_count)
    before = jnp.cumsum(flat_hits, axis=0) - flat_hits
    slot_pos = jnp.sum(before * flat_hits, axis=1).reshape(token_rows, choose_count)
    slot_ids = jnp.arange(capacity, dtype=jnp.int32)
    dispatch_table = onehot[:, :, :, None] * (slot_pos[:, :, None, None] == slot_ids).astype(
        jnp.float32
    )
    slot_table = jnp.sum(dispatch_table, axis=1).astype(jnp.bfloat16)
    packed_grad = jnp.einsum(
        "rec,rd->ecd", slot_table, grad_output, preferred_element_type=jnp.float32
    ).astype(jnp.bfloat16)
    packed_gate = jnp.einsum("rkec,rk->ec", dispatch_table, gate_low.astype(jnp.float32)).astype(
        jnp.bfloat16
    )
    send_grad = jnp.repeat(packed_grad, spread, axis=0)
    send_gate = jnp.repeat(packed_gate, spread, axis=0)
    recv_grad, recv_gate = (
        lax.all_to_all(send_grad, ("expert", "tensor"), split_axis=0, concat_axis=0, tiled=True),
        lax.all_to_all(send_gate, ("expert", "tensor"), split_axis=0, concat_axis=0, tiled=True),
    )
    recv_grad = recv_grad.reshape(sources * capacity, model_width)
    recv_gate = recv_gate.reshape(sources * capacity).astype(jnp.float32)
    hidden_rows = hidden[0]
    gated_grad = (recv_gate[:, None] * recv_grad.astype(jnp.float32)).astype(jnp.bfloat16)
    expert_image = lax.dot_general(
        recv_grad, down_weight, (((1,), (1,)), ((), ())), preferred_element_type=jnp.float32
    )
    hidden_part = (recv_gate[:, None] * expert_image).astype(jnp.bfloat16)
    gate_partial = jnp.sum(hidden_rows.astype(jnp.float32) * expert_image, axis=1).reshape(
        sources, capacity
    )
    returned = lax.all_to_all(
        gate_partial, ("expert", "tensor"), split_axis=0, concat_axis=0, tiled=True
    )
    expert_sums = jnp.sum(returned.reshape(expert_count, spread, capacity), axis=1)
    gate_grad = jnp.einsum("rkec,ec->rk", dispatch_table, expert_sums)
    mixed_term = jnp.sum(gate_values * gate_grad, axis=1, keepdims=True)
    logit_part = gate_values * (gate_grad - mixed_term)
    logit_grad = jnp.sum(onehot * logit_part[:, :, None], axis=1)
    input_grad = jnp.dot(
        logit_grad, router_weight.astype(jnp.float32).T, precision=lax.Precision.HIGHEST
    ).astype(jnp.bfloat16)
    router_local = jnp.dot(
        full_input.astype(jnp.float32).T, logit_grad, precision=lax.Precision.HIGHEST
    )
    router_grad = lax.psum(router_local, ("dp", "expert", "tensor"))
    hidden_all = lax.all_to_all(hidden_rows, "dp", split_axis=1, concat_axis=0, tiled=True)
    gated_all = lax.all_gather(gated_grad, "dp", axis=0, tiled=True)
    weight_sum = lax.dot_general(
        hidden_all, gated_all, (((0,), (0,)), ((), ())), preferred_element_type=jnp.float32
    ).astype(jnp.bfloat16)
    return (weight_sum, hidden_part[None], router_grad, input_grad)


def solution(mesh):
    return jax.shard_map(
        per_device,
        mesh=mesh,
        in_specs=(
            P(("dp", "expert"), "tensor"),
            P(),
            P(("dp", "expert", "tensor"), None),
            P(("expert", "tensor"), None),
            P("dp", None, ("expert", "tensor")),
            P(("dp", "expert", "tensor"), None),
        ),
        out_specs=(
            P(("expert", "tensor", "dp"), None),
            P("dp", None, ("expert", "tensor")),
            P(),
            P(("dp", "expert", "tensor"), None),
        ),
        check_vma=False,
    )
```

time: 40.1 us -> 35.1 us (0.88)
  Pallas kernels: 39.1 us -> 34.1 us
    pallas_call x1, Pallas kernels: 35.5 us -> 30 us  [by_kernels(): pl.pallas_call(functools.partial(exchange_kernel, groups, expert_ranks, t...]
    pallas_call x1, Pallas kernels: 3.57 us -> 4.11 us  [by_kernels(): pl.pallas_call(functools.partial(weight_kernel, tensor_ranks), out_shape=...]
where the time goes in v2:
time: 35.1 us; the launch traced here: 34.9 us
  Pallas kernels  34.1 us (97%)
  between operations  0.8 us (2%)
    pallas_call x1, Pallas kernels, by_kernels(): pl.pallas_call(functools.partial(exchange_kernel, groups, expert_ranks, t...  30 us
    pallas_call x1, Pallas kernels, by_kernels(): pl.pallas_call(functools.partial(weight_kernel, tensor_ranks), out_shape=...  4.11 us

profile of v2, /device:TPU:0, one launch (start us, length us, event | category | flops | bytes accessed | tf_op | source)
XLA Modules:
  0.0 34.9 jit_solution(15080637388827805276)
XLA Ops:
  0.6 30.0 %exchange.1 = (bf16[1152,2048]{1,0:T(8,128)(2,1)S(1)}, bf16[2,128,1920]{2,1,0:T(8,128)(2,1)S(1)}, bf16[2,128,2048]{2,1,0:T(8,128)(2,1)S(1)}, bf16[2,128,1920]{2,...) custom-call(s32[2,32]{1,0:T(2,128)} %bitcast.7, ...), custom_call_target="tpu_custom_call" | custom-call | tf_op jit(solution)/shard_map/exchange/pallas_call | solution.py:503
  30.7 4.1 %weight_grad.1 = (bf16[1920,2048]{1,0:T(8,128)(2,1)}, bf16[72,7680]{1,0:T(8,128)(2,1)}, bf16[32,2048]{1,0:T(8,128)(2,1)}, f32[8,2048]{1,0:T(8,128)}) custom-call(bf16[1152,2048]{1,0:T(8,128)(2,1)S(1)} %get-tuple-element.16.near_ref, bf16[2,128,1920]{2,1,0:T(8,128)(2,1)S(1)} %get-tuple-element.17.hidden_near, ...), custom_call_target="tpu_custom_call" | custom-call | tf_op jit(solution)/shard_map/weight_grad/pallas_call | solution.py:553

commit v3 on v2

--- a/solution.py
+++ b/solution.py
@@ -14,8 +14,9 @@
 VMEM_LIMIT = 50 * 1000 * 1000
 WEIGHT_LIMIT = 24 * 1000 * 1000
 OUT = pltpu.VMEM
-PAUSE = 8
-LAST_TILES = 2
+PAUSE = 6
+LAST_TILES = 4
+NEAR_FIFTHS = 3
 EXACT = lax.Precision.HIGHEST
 CONTRACT_LAST = (((1,), (1,)), ((), ()))
 CONTRACT_FIRST = (((0,), (0,)), ((), ()))
@@ -75,7 +76,8 @@
     trs = [(tensor + t) % tensor_ranks for t in range(tensor_ranks)]
     peers = [
         (ers[e] * tensor_ranks + trs[t], {"dp": group, "expert": ers[e], "tensor": trs[t]})
-        for e in range(expert_ranks) for t in range(tensor_ranks) if e or t
+        for e in sorted(range(expert_ranks), key=lambda e: abs(2 * e - expert_ranks))
+        for t in range(tensor_ranks) if e or t
     ]
     core = group % 2
     half = group // 2
@@ -120,7 +122,8 @@
     tail = hidden_near.shape[1] - slots
     for buffer in (hidden_near, hidden_far, gated_near, gated_far):
         buffer[:, slots:, :] = jnp.zeros((2, tail, buffer.shape[2]), bf16)
-    loads[0].wait()
+    for copy in loads[:4]:
+        copy.wait()
     labels = iota((experts, tokens), 0)
     pick_first = (ids_ref[0:1, :] == labels).astype(f32)
     pick_second = (ids_ref[1:2, :] == labels).astype(f32)
@@ -134,7 +137,6 @@
     table = jnp.where((hit > 0.5) & (jnp.abs(rank - slot) < 0.5), 1.0, 0.0).astype(f32)
     low_table = table.reshape(sources, PAD, tokens)[:, :HALF].reshape(sources * HALF, tokens)
     top_table = jnp.where((pick_both > 0.5) & (jnp.abs(before - HALF) < 0.5), 1.0, 0.0)
-    loads[1].wait()
     wide = send_low.shape[3]
     for h in range(2):
         send_low[h] = (
@@ -149,8 +151,6 @@
         top_table.astype(bf16), grad_ref[...], preferred_element_type=f32
     ).reshape(send_top.shape)
 
-    loads[2].wait()
-    loads[3].wait()
     own_weight = router_weight_ref[:, pl.ds(pl.multiple_of(tensor * span, LANES), span)]
 
     def part_logits(t):
@@ -171,12 +171,9 @@
         ).start()
     for to, where in peers:
         remote(
-            send_low.at[0, to], recv_low.at[0, source], low_send, low_recv.at[0], where
+            send_low.at[:, to], recv_low.at[:, source], low_send, low_recv, where
         ).start()
     for to, where in peers:
-        remote(
-            send_low.at[1, to], recv_low.at[1, source], low_send, low_recv.at[1], where
-        ).start()
         remote(send_top.at[to], recv_top.at[source], top_send, top_recv, where).start()
 
     hidden_to = (
@@ -246,8 +243,7 @@
         pull(c)
 
     drain(recv_info.at[pl.ds(0, sources - 1)], info_recv)
-    for h in range(2):
-        drain(recv_low.at[h, pl.ds(0, sources - 1)], low_recv.at[h])
+    drain(recv_low.at[:, pl.ds(0, sources - 1)], low_recv)
     drain(recv_top.at[pl.ds(0, sources - 1)], top_recv)
     model = packed.shape[1]
     for h in range(2):
@@ -541,7 +537,7 @@
             pltpu.VMEM((height, model), bf16),
             pltpu.VMEM((slots, model), f32),
             dma((5,)), dma((len(chunk_bounds(width // tile)),)), dma, dma,
-            dma, dma, dma, dma((2,)), dma, dma,
+            dma, dma, dma, dma, dma, dma,
             dma((3,)), dma((3,)), dma((3, 2)), dma((3, 2)), dma, dma,
             dma, dma, dma, dma, dma, dma, dma, dma,
         ],
@@ -573,7 +569,7 @@
 
 def near_rows(part):
     step = part_tile(part)
-    return part // step * 3 // 5 * step
+    return max(1, part // step * NEAR_FIFTHS // 5) * step
 
 
 def row_bounds(part):

time: 35.1 us -> 34.5 us (0.983)
  Pallas kernels: 34.1 us -> 33.6 us
    pallas_call x1, Pallas kernels: 30 us -> 29.5 us  [by_kernels(): pl.pallas_call(functools.partial(exchange_kernel, groups, expert_ranks, t...]
where the time goes in v3:
time: 34.5 us; the launch traced here: 34.4 us
  Pallas kernels  33.6 us (97%)
  between operations  0.8 us (2%)
    pallas_call x1, Pallas kernels, by_kernels(): pl.pallas_call(functools.partial(exchange_kernel, groups, expert_ranks, t...  29.5 us
    pallas_call x1, Pallas kernels, by_kernels(): pl.pallas_call(functools.partial(weight_kernel, tensor_ranks), out_shape=...  4.11 us

profile of v3, /device:TPU:0, one launch (start us, length us, event | category | flops | bytes accessed | tf_op | source)
XLA Modules:
  0.0 34.4 jit_solution(13109414263783108254)
XLA Ops:
  0.6 29.5 %exchange.1 = (bf16[1152,2048]{1,0:T(8,128)(2,1)S(1)}, bf16[2,128,1920]{2,1,0:T(8,128)(2,1)S(1)}, bf16[2,128,2048]{2,1,0:T(8,128)(2,1)S(1)}, bf16[2,128,1920]{2,...) custom-call(s32[2,32]{1,0:T(2,128)} %bitcast.7, ...), custom_call_target="tpu_custom_call" | custom-call | tf_op jit(solution)/shard_map/exchange/pallas_call | solution.py:499
  30.1 4.1 %weight_grad.1 = (bf16[1920,2048]{1,0:T(8,128)(2,1)}, bf16[72,7680]{1,0:T(8,128)(2,1)}, bf16[32,2048]{1,0:T(8,128)(2,1)}, f32[8,2048]{1,0:T(8,128)}) custom-call(bf16[1152,2048]{1,0:T(8,128)(2,1)S(1)} %get-tuple-element.16.near_ref, bf16[2,128,1920]{2,1,0:T(8,128)(2,1)S(1)} %get-tuple-element.17.hidden_near, ...), custom_call_target="tpu_custom_call" | custom-call | tf_op jit(solution)/shard_map/weight_grad/pallas_call | solution.py:549
